TPU v7x, 8 devices: a whole 2x2x1 slice. The times are simulated.
8 devices in a mesh: dp: 2 (over z, y), tp: 4 (over x, core).
Axes of the slice: x: 2, y: 2, z: 1, core: 2. Of those that a mesh axis runs over, the one named last changes fastest.
Arguments:
- hidden: bfloat16 [4, 256, 7168], P('dp', 'tp'), parts along dimension 0
- lengths: int32 [4], P('dp'), parts along dimension 0
- rope_cos: float32 [4, 256, 32], P('dp'), parts along dimension 0
- rope_sin: float32 [4, 256, 32], P('dp'), parts along dimension 0
- cache_lat: bfloat16 [4, 2304, 512], P('dp'), parts along dimension 0
- cache_pe: bfloat16 [4, 2304, 64], P('dp'), parts along dimension 0
- norm_in: float32 [7168], replicated
- w_dq: bfloat16 [7168, 1536], replicated
- norm_q: float32 [1536], replicated
- w_dkv: bfloat16 [7168, 576], replicated
- norm_kv: float32 [512], replicated
- w_uq: bfloat16 [1536, 64, 192], P(None, 'tp')
- w_uk: bfloat16 [512, 64, 128], P(None, 'tp')
- w_uv: bfloat16 [512, 64, 128], P(None, 'tp')
- w_out: bfloat16 [8192, 7168], P('tp')
Outputs:
- output 1: bfloat16 [4, 256, 7168], P('dp', 'tp'), parts along dimension 0
- output 2: bfloat16 [4, 2304, 512], P('dp'), parts along dimension 0
- output 3: bfloat16 [4, 2304, 64], P('dp'), parts along dimension 0
There are 2 independent parts. A program takes and returns all parts, laid end to end along the dimension named above; an argument that names none is the same for every part.
All inputs are finite; a program needn't handle non-finite values.
Results may differ from a plain program's by a relative error of at most 0.0160033.
Values are sent between devices in bfloat16 or wider.
A program may use at most 1 GiB of HBM per device.

v0:
```python
import jax
import jax.numpy as jnp
from jax import lax
from jax.sharding import PartitionSpec as P


def rms_norm(values, gain_vec):
    inv_rms = lax.rsqrt(jnp.mean(values * values, axis=-1, keepdims=True) + 1e-6)
    return values * inv_rms * gain_vec


def apply_rope(values, cos_tab, sin_tab):
    half_dim = values.shape[-1] // 2
    lower_half = values[..., :half_dim]
    upper_half = values[..., half_dim:]
    return jnp.concatenate([lower_half * cos_tab - upper_half * sin_tab, upper_half * cos_tab + lower_half * sin_tab], axis=-1)


def write_rows(old_rows, new_rows, start_row):
    return lax.dynamic_update_slice(old_rows, new_rows, (start_row, 0))


def solution(mesh):
    def local_step(hidden, lengths, rope_cos, rope_sin, cache_lat, cache_pe, norm_in, w_dq, norm_q, w_dkv, norm_kv, w_uq, w_uk, w_uv, w_out):
        gathered = lax.all_gather(hidden, "tp", axis=1, tiled=True)
        chunk_len = gathered.shape[1]
        model_dim = gathered.shape[2]
        kv_rank, heads_local, nope_dim = w_uk.shape
        value_dim = w_uv.shape[2]
        rope_dim = cache_pe.shape[2]
        cache_len = cache_lat.shape[1]
        normed = rms_norm(gathered.astype(jnp.float32), norm_in).astype(jnp.bfloat16)
        q_latent = rms_norm(jnp.einsum("btd,dq->btq", normed, w_dq, preferred_element_type=jnp.float32), norm_q).astype(jnp.bfloat16)
        kv_proj = jnp.einsum("btd,dk->btk", normed, w_dkv, preferred_element_type=jnp.float32)
        new_lat = rms_norm(kv_proj[..., :kv_rank], norm_kv).astype(jnp.bfloat16)
        new_pe = apply_rope(kv_proj[..., kv_rank:], rope_cos, rope_sin).astype(jnp.bfloat16)
        lat_all = jax.vmap(write_rows)(cache_lat, new_lat, lengths)
        pe_all = jax.vmap(write_rows)(cache_pe, new_pe, lengths)
        q_full = jnp.einsum("btq,qhd->bthd", q_latent, w_uq, preferred_element_type=jnp.float32)
        q_nope = q_full[..., :nope_dim].astype(jnp.bfloat16)
        q_pe = apply_rope(q_full[..., nope_dim:], rope_cos[:, :, None, :], rope_sin[:, :, None, :]).astype(jnp.bfloat16)
        keys_nope = jnp.einsum("bsc,chd->bshd", lat_all, w_uk, preferred_element_type=jnp.float32).astype(jnp.bfloat16)
        values_all = jnp.einsum("bsc,chv->bshv", lat_all, w_uv, preferred_element_type=jnp.float32).astype(jnp.bfloat16)
        scores = jnp.einsum("bthd,bshd->bhts", q_nope, keys_nope, preferred_element_type=jnp.float32)
        scores = scores + jnp.einsum("bthr,bsr->bhts", q_pe, pe_all, preferred_element_type=jnp.float32)
        key_pos = jnp.arange(cache_len)[None, None, :]
        row_limit = lengths[:, None, None] + jnp.arange(chunk_len)[None, :, None] + 1
        visible = (key_pos < row_limit)[:, None, :, :]
        scores = jnp.where(visible, scores * ((nope_dim + rope_dim) ** -0.5), -1e30)
        attn_probs = jax.nn.softmax(scores, axis=-1).astype(jnp.bfloat16)
        attn_out = jnp.einsum("bhts,bshv->bthv", attn_probs, values_all, preferred_element_type=jnp.float32).astype(jnp.bfloat16)
        out_heads = w_out.reshape(heads_local, value_dim, model_dim)
        head_sum = jnp.einsum("bthv,hvd->btd", attn_out, out_heads, preferred_element_type=jnp.float32)
        reduced = lax.psum_scatter(head_sum, "tp", scatter_dimension=1, tiled=True)
        return (reduced + hidden.astype(jnp.float32)).astype(jnp.bfloat16), lat_all, pe_all

    spec_tok = P("dp", "tp", None)
    spec_len = P("dp")
    spec_seq = P("dp", None, None)
    spec_vec = P(None)
    spec_mat = P(None, None)
    spec_head = P(None, "tp", None)
    spec_rows = P("tp", None)
    in_specs = (spec_tok, spec_len, spec_seq, spec_seq, spec_seq, spec_seq, spec_vec, spec_mat, spec_vec, spec_mat, spec_vec, spec_head, spec_head, spec_head, spec_rows)
    return jax.shard_map(local_step, mesh=mesh, in_specs=in_specs, out_specs=(spec_tok, spec_seq, spec_seq), check_vma=False)
```

profile of v0, /device:TPU:0, one launch (start us, length us, event | category | flops | bytes accessed | tf_op | source)
XLA Modules:
  0.0 438.7 jit_solution(10815954085003417022)
XLA Ops:
  7.2 0.0 all-gather.2.cloned.1.call-start
  7.3 5.0 %copy.70 = bf16[2,2304,512]{2,1,0:T(8,128)(2,1)} copy(bf16[2,2304,512]{2,1,0:T(8,128)(2,1)} %param.19) | data formatting | bytes 9437184
  12.2 0.0 all-gather.2.cloned.1.call-update
  12.2 0.0 reduce-scatter.2.cloned.1.call-start
  12.3 0.1 pad_clamp_fusion
  12.4 0.1 copy.18
  12.5 0.1 add_add_fusion
  12.6 1.7 iota_compare_fusion
  14.3 50.6 %all-gather.2.cloned.1.call-done = bf16[2,256,7168]{2,1,0:T(8,128)(2,1)} async-done(((bf16[2,64,7168]{2,1,0:T(8,128)(2,1)}), bf16[2,256,7168]{2,1,0:T(8,128)(2,1)}) %all-gather.2.cloned.1.call-update) | async-done | bytes 7340048 | tf_op jit(solution)/shard_map/all_gather | solution.py:25
  64.9 4.7 %fusion.10 = f32[2,256]{1,0:T(2,128)S(1)} fusion(bf16[2,256,7168]{2,1,0:T(8,128)(2,1)} %all-gather.2.cloned.1.call-done), kind=kLoop, calls=%fused_computation.22 | loop fusion | flops 11009536 | bytes 7342080 | tf_op jit(solution)/shard_map/reduce_sum | solution.py:8
  69.7 0.4 copy-done.2
  70.1 7.1 %fusion.15 = f32[2,256,576]{1,2,0:T(8,128)S(1)} fusion(bf16[7168,576]{0,1:T(8,128)(2,1)} %param.24, bf16[2,256,7168]{2,1,0:T(8,128)(2,1)S(1)} %copy-done.2, f32[7168]{0:T(1024)S(1)} %copy-done.16, f32[2,256]{1,0:T(2,128)S(1)} %add_rsqrt_fusion.2), kind=kOutput, calls=%fused_computation.28 | convolution fusion | flops 4242538496 | bytes 16807936 | tf_op jit(solution)/shard_map/btd,dk->btk/dot_general | solution.py:34
  77.2 0.1 multiply_reduce_fusion.1
  77.3 0.9 copy-done.3
  78.3 14.2 %while.3 = (s32[]{:T(128)}, bf16[2,2304,64]{1,2,0:T(8,128)(2,1)S(1)}, s32[2,3]{1,0:T(2,128)S(1)}, bf16[2,256,64]{1,2,0:T(8,128)(2,1)S(1)}, s32[]{:T(128)}, /*index=5*/s32[3]{0:T(128)S(1)}, s32[]{:T(128)}) while((s32[]{:T(128)}, bf16[2,2304,64]{1,2,0:T(8,128)(2,1)S(1)}, s32[2,3]{1,0:T(2,128)S(1)}, bf16[2,256,64]{1,2,0:T(8,128)(2,1)S(1)}, s32[]{:T(128)}, ...), condition=%wide.while_cond.1, body=%wide.while_body.1.sunk | while | flops 16403 | bytes 164011 | solution.py:20
  78.3 0.6 fusion.64
  79.0 2.6 and_reduce_fusion.5
  81.6 2.0 dynamic-slice_select_fusion.5
  83.6 1.6 dynamic-update-slice.7
  85.3 0.6 fusion.64
  85.9 2.6 and_reduce_fusion.5
  88.5 2.0 dynamic-slice_select_fusion.5
  90.6 1.9 dynamic-update-slice.7
  92.5 17.7 %multiply_reduce_fusion = (f32[2,256]{1,0:T(2,128)S(1)}, f32[2,256,1536]{2,1,0:T(8,128)S(1)}) fusion(bf16[7168,1536]{1,0:T(8,128)(2,1)} %param.22, bf16[2,256,7168]{2,1,0:T(8,128)(2,1)} %all-gather.2.cloned.1.call-done, f32[7168]{0:T(1024)S(1)} %copy-done.16, f32[2,256]{1,0:T(2,128)S(1)} %add_rsqrt_fusion.2), kind=kOutput, calls=%fused_computation.37 | convolution fusion | flops 11290542080 | bytes 32538624 | tf_op jit(solution)/shard_map/btd,dq->btq/dot_general | solution.py:33
  110.3 8.0 %fusion.13 = f32[2,256,16,192]{1,3,2,0:T(8,128)S(1)} fusion(bf16[1536,16,192]{0,2,1:T(8,128)(2,1)} %param.26, f32[2,256,1536]{2,1,0:T(8,128)S(1)} %get-tuple-element.54, f32[1536]{0:T(1024)S(1)} %copy-done.17, f32[2,256]{1,0:T(2,128)S(1)} %add_rsqrt_fusion), kind=kOutput, calls=%fused_computation.26 | convolution fusion | flops 4834197504 | bytes 18882560 | tf_op jit(solution)/shard_map/btq,qhd->bthd/dot_general | solution.py:39
  118.2 1.6 subtract_convert_fusion
  119.9 0.2 multiply_convert_fusion.1
  120.1 1.1 copy-done.9
  121.1 20.3 %while.2 = (s32[]{:T(128)}, bf16[2,2304,512]{2,1,0:T(8,128)(2,1)}, s32[2,3]{1,0:T(2,128)S(1)}, bf16[2,256,512]{1,2,0:T(8,128)(2,1)S(1)}, s32[]{:T(128)}, /*index=5*/s32[3]{0:T(128)S(1)}, s32[]{:T(128)}) while((s32[]{:T(128)}, bf16[2,2304,512]{2,1,0:T(8,128)(2,1)}, s32[2,3]{1,0:T(2,128)S(1)}, bf16[2,256,512]{1,2,0:T(8,128)(2,1)S(1)}, s32[]{:T(128)}, ...), condition=%wide.while_cond, body=%wide.while_body.sunk | while | flops 131091 | bytes 2359467 | solution.py:20
  121.1 0.7 fusion.63
  121.8 2.7 and_reduce_fusion.4
  124.5 0.1 copy.53
  124.6 3.0 dynamic-slice_select_fusion.4
  127.6 3.2 dynamic-update-slice.6
  130.8 0.7 fusion.63
  131.5 2.7 and_reduce_fusion.4
  134.2 0.1 copy.53
  134.3 3.0 dynamic-slice_select_fusion.4
  137.3 4.1 dynamic-update-slice.6
  141.4 16.5 %fusion.21 = bf16[2,2304,16,128]{3,1,2,0:T(8,128)(2,1)} fusion(bf16[2,2304,512]{2,1,0:T(8,128)(2,1)} %get-tuple-element.8, bf16[512,16,128,1]{2,1,0,3:T(8,128)(2,1)} %bitcast.91), kind=kOutput, calls=%fused_computation.31 | convolution fusion | flops 9663676416 | bytes 25690112 | tf_op jit(solution)/shard_map/bsc,chv->bshv/dot_general | solution.py:43
  157.9 20.9 %copy.46 = bf16[2,2304,16,128]{3,2,1,0:T(8,128)(2,1)} copy(bf16[2,2304,16,128]{3,1,2,0:T(8,128)(2,1)} %fusion.21) | data formatting | bytes 37748736 | tf_op jit(solution)/shard_map/bsc,chv->bshv/dot_general | solution.py:43
  178.8 28.0 %fusion.36 = f32[2,2304,256,16]{1,2,3,0:T(8,128)} fusion(bf16[2,256,16,32]{1,3,2,0:T(8,128)(2,1)} %get-tuple-element.50, bf16[2,256,16,32]{1,3,2,0:T(8,128)(2,1)S(1)} %copy-done.8, bf16[2,2304,64]{1,2,0:T(8,128)(2,1)S(1)} %copy-done.6), kind=kOutput, calls=%fused_computation.45 | convolution fusion | flops 2418016256 | bytes 77135872 | tf_op jit(solution)/shard_map/bthr,bsr->bhts/dot_general | solution.py:45
  206.8 64.6 %fusion.45 = (f32[2,16,256]{2,1,0:T(8,128)S(1)}, f32[2,16,256,2304]{3,2,1,0:T(8,128)}) fusion(f32[2,2304,256,16]{1,2,3,0:T(8,128)} %fusion.36, pred[2,256,2304]{2,1,0:T(8,128)(4,1)} %iota_compare_fusion, bf16[2,2304,512]{2,1,0:T(8,128)(2,1)} %get-tuple-element.8, f32[2,256,16,192]{1,3,2,0:T(8,128)} %copy-done.9, bf16[512,16,128,1]{2,1,0,3:T(8,128)(2,1)S(1)} %bitcast.89), kind=kOutput, calls=%fused_computation.68 | convolution fusion | flops 14599325696 | bytes 161120256 | tf_op jit(solution)/shard_map/sub | solution.py:50
  271.4 31.4 %fusion.59 = bf16[2,256,16,128]{3,1,2,0:T(8,128)(2,1)S(1)} fusion(bf16[2,2304,16,128]{3,2,1,0:T(8,128)(2,1)} %copy.46, f32[2,16,256,2304]{3,2,1,0:T(8,128)} %get-tuple-element.56, f32[2,16,256]{2,1,0:T(8,128)S(1)} %get-tuple-element.55), kind=kOutput, calls=%fused_computation.38.clone.1 | convolution fusion | flops 4870635520 | bytes 96501760 | tf_op jit(solution)/shard_map/bhts,bshv->bthv/dot_general | solution.py:51
  302.9 21.4 %convolution_bitcast_fusion = f32[2,256,7168]{2,1,0:T(8,128)} fusion(bf16[16,128,7168,1]{2,1,0,3:T(8,128)(2,1)} %bitcast.90, bf16[2,256,16,128]{3,1,2,0:T(8,128)(2,1)S(1)} %fusion.59), kind=kOutput, calls=%fused_computation.25 | convolution fusion | flops 15032385536 | bytes 46137344 | tf_op jit(solution)/shard_map/bthv,hvd->btd/dot_general | solution.py:53
  324.3 0.0 reduce-scatter.2.cloned.1.call-update
  324.3 103.4 %reduce-scatter.2.cloned.1.call-done = f32[2,64,7168]{2,1,0:T(8,128)} async-done(((f32[2,256,7168]{2,1,0:T(8,128)}), f32[2,64,7168]{2,1,0:T(8,128)}) %reduce-scatter.2.cloned.1.call-update) | async-done | bytes 3670032 | tf_op jit(solution)/shard_map/reduce_scatter | solution.py:54
  427.7 4.2 add_convert_fusion
  (47 shorter events, 0.2 us)
Async XLA Ops:
  7.2 199.7 %copy-start = (bf16[512,16,128]{2,1,0:T(8,128)(2,1)S(1)}, bf16[512,16,128]{2,1,0:T(8,128)(2,1)}, u32[]{:S(2)}) copy-start(bf16[512,16,128]{2,1,0:T(8,128)(2,1)} %param.27) | copy-start | bytes 6291460
  7.2 5.1 %copy-start.15 = (s32[2]{0:T(128)S(1)}, s32[2]{0:T(128)}, u32[]{:S(2)}) copy-start(s32[2]{0:T(128)} %constant.14.clone.1) | copy-start | bytes 28
  7.2 5.1 %copy-start.14 = (s32[2]{0:T(128)S(1)}, s32[2]{0:T(128)}, u32[]{:S(2)}) copy-start(s32[2]{0:T(128)} %param.16) | copy-start | bytes 28
  7.2 57.7 %all-gather.2.cloned.1.call-start = ((), (), s32[]{:S(2)}) async-start(), calls=%async_computation.1 | async-start | bytes 9175040 | tf_op jit(solution)/shard_map/all_gather | solution.py:25
  12.2 57.4 %copy-start.16 = (f32[7168]{0:T(1024)S(1)}, f32[7168]{0:T(1024)}, u32[]{:S(2)}) copy-start(f32[7168]{0:T(1024)} %param.21) | copy-start | bytes 86020
  12.2 415.5 %reduce-scatter.2.cloned.1.call-start = ((), (), s32[]{:S(2)}) async-start(), calls=%async_computation.2 | async-start | bytes 18350080 | tf_op jit(solution)/shard_map/reduce_scatter | solution.py:54
  64.9 5.2 %copy-start.2 = (bf16[2,256,7168]{2,1,0:T(8,128)(2,1)S(1)}, bf16[2,256,7168]{2,1,0:T(8,128)(2,1)}, u32[]{:S(2)}) copy-start(bf16[2,256,7168]{2,1,0:T(8,128)(2,1)} %all-gather.2.cloned.1.call-done) | copy-start | bytes 22020100
  70.1 8.2 %copy-start.10 = (f32[2,256,32]{1,2,0:T(8,128)S(1)}, f32[2,256,32]{1,2,0:T(8,128)}, u32[]{:S(2)}) copy-start(f32[2,256,32]{1,2,0:T(8,128)} %param.18) | copy-start | bytes 196612
  70.1 8.2 %copy-start.11 = (f32[2,256,32]{1,2,0:T(8,128)S(1)}, f32[2,256,32]{1,2,0:T(8,128)}, u32[]{:S(2)}) copy-start(f32[2,256,32]{1,2,0:T(8,128)} %param.17) | copy-start | bytes 196612
  70.1 8.2 %copy-start.7 = (bf16[2,2304,64]{1,2,0:T(8,128)(2,1)S(1)}, bf16[2,2304,64]{1,2,0:T(8,128)(2,1)}, u32[]{:S(2)}) copy-start(bf16[2,2304,64]{1,2,0:T(8,128)(2,1)} %param.20) | copy-start | bytes 1769476
  70.1 8.2 %copy-start.12 = (s32[3]{0:T(128)S(1)}, s32[3]{0:T(128)}, u32[]{:S(2)}) copy-start(s32[3]{0:T(128)} %constant.104) | copy-start | bytes 40
  77.2 1.0 copy-start.3
  92.5 17.7 %copy-start.5 = (bf16[2,2304,64]{1,2,0:T(8,128)(2,1)}, bf16[2,2304,64]{1,2,0:T(8,128)(2,1)S(1)}, u32[]{:S(2)}) copy-start(bf16[2,2304,64]{1,2,0:T(8,128)(2,1)S(1)} %get-tuple-element.16) | copy-start | bytes 1769476
  92.5 17.7 %copy-start.17 = (f32[1536]{0:T(1024)S(1)}, f32[1536]{0:T(1024)}, u32[]{:S(2)}) copy-start(f32[1536]{0:T(1024)} %param.23) | copy-start | bytes 18436
  110.2 9.7 %copy-start.4 = (f32[2,256,576]{1,2,0:T(8,128)S(1)}, f32[2,256,576]{1,2,0:T(8,128)}, u32[]{:S(2)}) copy-start(f32[2,256,576]{1,2,0:T(8,128)} %copy-done.3) | copy-start | bytes 3538948
  110.2 9.6 %copy-start.13 = (f32[512]{0:T(512)S(1)}, f32[512]{0:T(512)}, u32[]{:S(2)}) copy-start(f32[512]{0:T(512)} %param.25) | copy-start | bytes 6148
  118.2 2.9 copy-start.9
  157.9 20.9 %copy-start.6 = (bf16[2,2304,64]{1,2,0:T(8,128)(2,1)S(1)}, bf16[2,2304,64]{1,2,0:T(8,128)(2,1)}, u32[]{:S(2)}) copy-start(bf16[2,2304,64]{1,2,0:T(8,128)(2,1)} %copy-done.5) | copy-start | bytes 1769476
  157.9 20.9 %copy-start.8 = (bf16[2,256,16,32]{1,3,2,0:T(8,128)(2,1)S(1)}, bf16[2,256,16,32]{1,3,2,0:T(8,128)(2,1)}, u32[]{:S(2)}) copy-start(bf16[2,256,16,32]{1,3,2,0:T(8,128)(2,1)} %get-tuple-element.49) | copy-start | bytes 1572868
  324.3 107.6 %copy-start.1 = (bf16[512,16,128]{2,1,0:T(8,128)(2,1)S(1)}, bf16[512,16,128]{2,1,0:T(8,128)(2,1)}, u32[]{:S(2)}) copy-start(bf16[512,16,128]{2,1,0:T(8,128)(2,1)} %param.27) | copy-start | bytes 6291460
Sparse Core Ops, SparseCore 0:
  12.4 52.4 all-gather.1
  324.4 103.2 reduce-scatter.1
where the time goes:
time: 440 us; the launch traced here: 439 us
  matrix products  195 us (44%)
  waiting for transfers between devices  154 us (35%)
  local copies, waits for them, and re-layouts  42.2 us (10%)
  other arithmetic  33.4 us (8%)
  between operations  14.3 us (3%)
    reduce_scatter x1, waiting for transfers between devices, local_step(): reduced = lax.psum_scatter(head_sum, 'tp', scatter_dimension=1, tiled=True)  103 us
    sub x1, matrix products, local_step(): attn_probs = jax.nn.softmax(scores, axis=-1).astype(jnp.bfloat16)  64.6 us
    all_gather x1, waiting for transfers between devices, local_step(): gathered = lax.all_gather(hidden, 'tp', axis=1, tiled=True)  50.6 us
    dot_general x1, matrix products, local_step(): jnp.einsum('bhts,bshv->bthv', attn_probs, values_all, preferred_element_t...  31.4 us
    dot_general x1, matrix products, local_step(): jnp.einsum('bthr,bsr->bhts', q_pe, pe_all, preferred_element_type=jnp.flo...  28 us
    dot_general x1, matrix products, local_step(): jnp.einsum('bthv,hvd->btd', attn_out, out_heads, preferred_element_type=j...  21.4 us
    dot_general x1, local copies, waits for them, and re-layouts, local_step(): jnp.einsum('bsc,chv->bshv', lat_all, w_uv, preferred_element_type=jnp.flo...  20.9 us
    scatter x8, other arithmetic  20.6 us
  transfers between devices with their start and end apart: 2, of which 2 were waited for; matrix products, arithmetic and copies ran while one was open for 0% of the time, Pallas kernels for 0%

commit v1 on v0

v1 whole, which is shorter than its diff:
```python
import functools

import jax
import jax.numpy as jnp
from jax import lax
from jax.experimental import pallas as pl
from jax.experimental.pallas import tpu as pltpu
from jax.sharding import PartitionSpec as P

F32 = jnp.float32
BF16 = jnp.bfloat16
EPS = 1e-6
MIB = 1 << 20
LAT_W = 2176
PREFIX = 2048
ROW_BLK = 512
SCALE = 192.0 ** -0.5
LOG2E = 1.4426950408889634
NT = (((1,), (1,)), ((), ()))


def dot(lhs, rhs):
    return jnp.dot(lhs, rhs, preferred_element_type=F32)


def dot_nt(lhs, rhs):
    return lax.dot_general(lhs, rhs, NT, preferred_element_type=F32)


def cost(flops, nbytes):
    return pl.CostEstimate(flops=int(flops), bytes_accessed=int(nbytes), transcendentals=0)


def proj_kernel(x_ref, g1_ref, wq_ref, wkvt_ref, gq_ref, gkv_ref, cos_ref, sin_ref, out_ref, a_s, q_acc, kv_acc):
    step = pl.program_id(0)
    depth = wq_ref.shape[0]

    @pl.when(step == 0)
    def _():
        xf = x_ref[...].astype(F32)
        inv = lax.rsqrt(jnp.mean(xf * xf, axis=-1, keepdims=True) + EPS)
        a_s[...] = (x_ref[...].astype(F32) * inv * g1_ref[...]).astype(BF16)
        q_acc[...] = jnp.zeros_like(q_acc)
        kv_acc[...] = jnp.zeros_like(kv_acc)

    a_blk = a_s[:, pl.ds(pl.multiple_of(step * depth, 128), depth)]
    q_acc[...] += dot(a_blk, wq_ref[...])
    kv_acc[...] += dot_nt(a_blk, wkvt_ref[...])

    @pl.when(step == pl.num_programs(0) - 1)
    def _():
        q = q_acc[...]
        inv = lax.rsqrt(jnp.mean(q * q, axis=-1, keepdims=True) + EPS)
        out_ref[:, :1536] = (q * inv * gq_ref[...]).astype(BF16)
        c = kv_acc[:, :512]
        inv = lax.rsqrt(jnp.mean(c * c, axis=-1, keepdims=True) + EPS)
        out_ref[:, 1536:2048] = (c * inv * gkv_ref[...]).astype(BF16)
        v1 = kv_acc[:, 512:544]
        v2 = kv_acc[:, 544:576]
        cos = cos_ref[...]
        sin = sin_ref[...]
        rot = jnp.concatenate([v1 * cos - v2 * sin, v2 * cos + v1 * sin, jnp.zeros((v1.shape[0], 64), F32)], axis=1)
        out_ref[:, 2048:] = rot.astype(BF16)


def project(x, g1, w_dq, w_dkvt, g_q, g_kv, cos, sin):
    rows, dim = x.shape
    depth = 1024
    const = lambda shape: pl.BlockSpec(shape, lambda k: (0,) * len(shape))
    return pl.pallas_call(
        proj_kernel,
        grid=(dim // depth,),
        in_specs=[
            const((rows, dim)),
            const((1, dim)),
            pl.BlockSpec((depth, 1536), lambda k: (k, 0)),
            pl.BlockSpec((576, depth), lambda k: (0, k)),
            const((1, 1536)),
            const((1, 512)),
            const((rows, 32)),
            const((rows, 32)),
        ],
        out_specs=const((rows, LAT_W)),
        out_shape=jax.ShapeDtypeStruct((rows, LAT_W), BF16),
        scratch_shapes=[pltpu.VMEM((rows, dim), BF16), pltpu.VMEM((rows, 1536), F32), pltpu.VMEM((rows, 576), F32)],
        compiler_params=pltpu.CompilerParams(vmem_limit_bytes=40 * MIB),
        cost_estimate=cost(2 * rows * dim * 2112 * 3, dim * 2112 * 2),
        name="project",
    )(x, g1, w_dq, w_dkvt, g_q, g_kv, cos, sin)


def prep_kernel(wuk_ref, wuv_ref, wk_ref, wvt_ref):
    wk_ref[...] = wuk_ref[...].reshape(wk_ref.shape)
    wvt_ref[...] = wuv_ref[...].reshape(wk_ref.shape).T


def prep_weights(w_uk, w_uv):
    rank, heads, dim = w_uk.shape
    blk = 256
    spec = pl.BlockSpec((blk, heads, dim), lambda i: (i, 0, 0))
    return pl.pallas_call(
        prep_kernel,
        grid=(rank // blk,),
        in_specs=[spec, spec],
        out_specs=[pl.BlockSpec((blk, heads * dim), lambda i: (i, 0)), pl.BlockSpec((heads * dim, blk), lambda i: (0, i))],
        out_shape=[jax.ShapeDtypeStruct((rank, heads * dim), BF16), jax.ShapeDtypeStruct((heads * dim, rank), BF16)],
        compiler_params=pltpu.CompilerParams(vmem_limit_bytes=40 * MIB),
        cost_estimate=cost(4e9, 8 * MIB),
        name="prep",
    )(w_uk, w_uv)


def kv_kernel(seq, len_ref, c_ref, wk_ref, wvt_ref, k_ref, vt_ref):
    @pl.when(pl.program_id(0) * ROW_BLK < len_ref[seq])
    def _():
        c = c_ref[...]
        k_ref[...] = dot(c, wk_ref[...]).astype(BF16)
        vt_ref[...] = dot_nt(wvt_ref[...], c).astype(BF16)

    @pl.when(pl.program_id(0) * ROW_BLK >= len_ref[seq])
    def _():
        vt_ref[...] = jnp.zeros_like(vt_ref)


def kv_up(seq, lengths, cache_lat, wk, wvt):
    rank, width = wk.shape
    blocks = PREFIX // ROW_BLK
    last = lambda r, n: jnp.minimum(r, (n[seq] + ROW_BLK - 1) // ROW_BLK - 1)
    grid_spec = pltpu.PrefetchScalarGridSpec(
        num_scalar_prefetch=1,
        grid=(blocks,),
        in_specs=[
            pl.BlockSpec((None, ROW_BLK, rank), lambda r, n: (seq, last(r, n), 0)),
            pl.BlockSpec((rank, width), lambda r, n: (0, 0)),
            pl.BlockSpec((width, rank), lambda r, n: (0, 0)),
        ],
        out_specs=[
            pl.BlockSpec((ROW_BLK, width), lambda r, n: (last(r, n), 0)),
            pl.BlockSpec((width, ROW_BLK), lambda r, n: (0, r)),
        ],
    )
    return pl.pallas_call(
        functools.partial(kv_kernel, seq),
        grid_spec=grid_spec,
        out_shape=[jax.ShapeDtypeStruct((PREFIX, width), BF16), jax.ShapeDtypeStruct((width, PREFIX), BF16)],
        compiler_params=pltpu.CompilerParams(vmem_limit_bytes=48 * MIB),
        cost_estimate=cost(4 * PREFIX * rank * width * 2, 20 * MIB),
        name="kv_up",
    )(lengths, cache_lat, wk, wvt)


def attn_kernel(seq, len_ref, place_ref, b0, b1, b2, b3, cos_ref, sin_ref, pet_ref, wuqt_ref, wk_ref, wvt_ref, k_ref, vt_ref,
                o_ref, cnew_ref, knewt_ref, cqt, cn, cnt, kn, pe):
    step = pl.program_id(0)

    @pl.when(step == 0)
    def _():
        for k, blk in enumerate((b0, b1, b2, b3)):
            rows = pl.ds(pl.multiple_of(place_ref[k], 64), 64)
            cnew_ref[rows, :] = blk[:, 1536:2048]
            cn[rows, :] = blk[:, 1536:2048]
            kn[rows, :] = blk[:, 2048:]
            cqt[rows, :] = blk[:, :1536]
        cnt[...] = cn[...].T
        knewt_ref[...] = kn[...].T[:64]
        pe[...] = pet_ref[:, :PREFIX].T

    @pl.when(len_ref[seq] >= 0)
    def _():
        length = len_ref[seq]
        cos = cos_ref[...]
        sin = sin_ref[...]
        row_old = lax.broadcasted_iota(jnp.int32, (PREFIX, 256), 0)
        row_new = lax.broadcasted_iota(jnp.int32, (256, 256), 0)
        col_new = lax.broadcasted_iota(jnp.int32, (256, 256), 1)
        c2 = SCALE * LOG2E
        for h in range(2):
            d = slice(128 * h, 128 * h + 128)
            q = dot_nt(wuqt_ref[h], cqt[...])
            v1 = q[128:160]
            v2 = q[160:192]
            qt = jnp.concatenate([q[:128], v1 * cos - v2 * sin, v2 * cos + v1 * sin], axis=0).astype(BF16)
            k_new = dot(cn[...], wk_ref[:, d]).astype(BF16)
            vt_new = dot(wvt_ref[d, :], cnt[...]).astype(BF16)
            s_old = dot(jnp.concatenate([k_ref[:, d], pe[...]], axis=1), qt)
            s_new = dot(jnp.concatenate([k_new, kn[:, :64]], axis=1), qt)
            s_old = jnp.where(row_old < length, s_old * c2, -1e30)
            s_new = jnp.where(row_new <= col_new, s_new * c2, -1e30)
            m = jnp.maximum(jnp.max(s_old, axis=0, keepdims=True), jnp.max(s_new, axis=0, keepdims=True))
            p_old = jnp.exp2(s_old - m)
            p_new = jnp.exp2(s_new - m)
            inv = 1.0 / (jnp.sum(p_old, axis=0, keepdims=True) + jnp.sum(p_new, axis=0, keepdims=True))
            p_old = jnp.where(row_old < length, p_old * inv, 0.0).astype(BF16)
            ot = dot(vt_ref[d, :], p_old) + dot(vt_new, (p_new * inv).astype(BF16))
            o_ref[:, d] = ot.T.astype(BF16)


def attend(seq, lengths, place, blocks, cos_t, sin_t, pe_t, w_uqt, wk, wvt, k_old, vt_old):
    lat_spec = pl.BlockSpec((None, 64, LAT_W), lambda h, n, p: (seq, 0, 0))
    grid_spec = pltpu.PrefetchScalarGridSpec(
        num_scalar_prefetch=2,
        grid=(8,),
        in_specs=[lat_spec] * 4 + [
            pl.BlockSpec((None, 32, 256), lambda h, n, p: (seq, 0, 0)),
            pl.BlockSpec((None, 32, 256), lambda h, n, p: (seq, 0, 0)),
            pl.BlockSpec((None, 64, 2304), lambda h, n, p: (seq, 0, 0)),
            pl.BlockSpec((2, 192, 1536), lambda h, n, p: (h, 0, 0)),
            pl.BlockSpec((512, 256), lambda h, n, p: (0, h)),
            pl.BlockSpec((256, 512), lambda h, n, p: (h, 0)),
            pl.BlockSpec((PREFIX, 256), lambda h, n, p: (0, h)),
            pl.BlockSpec((256, PREFIX), lambda h, n, p: (h, 0)),
        ],
        out_specs=[
            pl.BlockSpec((256, 256), lambda h, n, p: (0, h)),
            pl.BlockSpec((256, 512), lambda h, n, p: (0, 0)),
            pl.BlockSpec((64, 256), lambda h, n, p: (0, 0)),
        ],
        scratch_shapes=[
            pltpu.VMEM((256, 1536), BF16),
            pltpu.VMEM((256, 512), BF16),
            pltpu.VMEM((512, 256), BF16),
            pltpu.VMEM((256, 128), BF16),
            pltpu.VMEM((PREFIX, 64), BF16),
        ],
    )
    return pl.pallas_call(
        functools.partial(attn_kernel, seq),
        grid_spec=grid_spec,
        out_shape=[
            jax.ShapeDtypeStruct((256, 2048), BF16),
            jax.ShapeDtypeStruct((256, 512), BF16),
            jax.ShapeDtypeStruct((64, 256), BF16),
        ],
        compiler_params=pltpu.CompilerParams(vmem_limit_bytes=56 * MIB),
        cost_estimate=cost(16 * 256 * 2304 * 1024 * 2, 32 * MIB),
        name="attend",
    )(lengths, place, *blocks, cos_t, sin_t, pe_t, w_uqt, wk, wvt, k_old, vt_old)


def out_kernel(rows_ref, o_ref, w_ref, mine_ref, sib_ref):
    r0 = pl.multiple_of(rows_ref[0], 64)
    r1 = pl.multiple_of(rows_ref[1], 64)
    lhs = jnp.concatenate([o_ref[pl.ds(r0, 64), :], o_ref[pl.ds(r1, 64), :]], axis=0)
    y = dot(lhs, w_ref[...])
    mine_ref[...] = y[:64]
    sib_ref[...] = y[64:]


def out_proj(rows, o, w_out, half):
    cols = 512
    steps = 7
    grid_spec = pltpu.PrefetchScalarGridSpec(
        num_scalar_prefetch=1,
        grid=(steps,),
        in_specs=[
            pl.BlockSpec((256, 2048), lambda n, r: (0, 0)),
            pl.BlockSpec((2048, cols), lambda n, r: (0, n + half * steps)),
        ],
        out_specs=[pl.BlockSpec((64, cols), lambda n, r: (0, n))] * 2,
    )
    shape = jax.ShapeDtypeStruct((64, cols * steps), F32)
    return pl.pallas_call(
        out_kernel,
        grid_spec=grid_spec,
        out_shape=[shape, shape],
        compiler_params=pltpu.CompilerParams(vmem_limit_bytes=40 * MIB),
        cost_estimate=cost(2 * 128 * 2048 * 3584 * 3, 16 * MIB),
        name="out_proj",
    )(rows, o, w_out)


def solution(mesh):
    def local_step(hidden, lengths, rope_cos, rope_sin, cache_lat, cache_pe, norm_in, w_dq, norm_q, w_dkv, norm_kv, w_uq, w_uk, w_uv, w_out):
        me = lax.axis_index("tp")
        swap = lambda v, bit: lax.ppermute(v, "tp", [(i, i ^ bit) for i in range(4)])
        cos_t = jnp.swapaxes(rope_cos, 1, 2)
        sin_t = jnp.swapaxes(rope_sin, 1, 2)
        pe_t = jnp.swapaxes(cache_pe, 1, 2)
        w_uqt = jnp.transpose(w_uq, (1, 2, 0))
        own = lambda tab: lax.dynamic_slice_in_dim(tab, me * 64, 64, axis=1).reshape(128, 32)
        lat = project(hidden.reshape(128, -1), norm_in[None], w_dq, w_dkv.T, norm_q[None], norm_kv[None], own(rope_cos), own(rope_sin))
        lat = lat.reshape(2, 64, LAT_W)
        far = swap(lat, 2)
        near = swap(lat, 1)
        wk, wvt = prep_weights(w_uk, w_uv)
        k_old, vt_old = kv_up(0, lengths, cache_lat, wk, wvt)
        diag = swap(far, 1)
        place = jnp.stack([me, me ^ 1, me ^ 2, me ^ 3]).astype(jnp.int32) * 64
        rows_far = place[2:]
        rows_own = place[:2]
        blocks = (lat, near, far, diag)
        o0, c0, p0 = attend(0, lengths, place, blocks, cos_t, sin_t, pe_t, w_uqt, wk, wvt, k_old, vt_old)

        def far_sum(o):
            got = []
            for half in range(2):
                mine, sib = out_proj(rows_far, o, w_out, half)
                got.append(swap(mine + swap(sib, 1), 2))
            return got

        got0 = far_sum(o0)
        lengths_b, _ = lax.optimization_barrier((lengths, o0[0, 0]))
        k_old, vt_old = kv_up(1, lengths_b, cache_lat, wk, wvt)
        o1, c1, p1 = attend(1, lengths, place, blocks, cos_t, sin_t, pe_t, w_uqt, wk, wvt, k_old, vt_old)
        got1 = far_sum(o1)

        def own_sum(o, x, got):
            parts = []
            for half in range(2):
                mine, sib = out_proj(rows_own, o, w_out, half)
                cols = slice(half * 3584, half * 3584 + 3584)
                parts.append((x[:, cols].astype(F32) + (mine + swap(sib, 1) + got[half])).astype(BF16))
            return jnp.concatenate(parts, axis=1)

        y = jnp.stack([own_sum(o0, hidden[0], got0), own_sum(o1, hidden[1], got1)])
        zero = jnp.zeros((), jnp.int32)
        lat_new = cache_lat
        pe_new = pe_t
        for b, (c, p) in enumerate(((c0, p0), (c1, p1))):
            lat_new = lax.dynamic_update_slice(lat_new, c[None], (jnp.int32(b), lengths[b], zero))
            pe_new = lax.dynamic_update_slice(pe_new, p[None], (jnp.int32(b), zero, lengths[b]))
        return y, lat_new, jnp.swapaxes(pe_new, 1, 2)

    spec_tok = P("dp", "tp", None)
    spec_len = P("dp")
    spec_seq = P("dp", None, None)
    spec_vec = P(None)
    spec_mat = P(None, None)
    spec_head = P(None, "tp", None)
    spec_rows = P("tp", None)
    in_specs = (spec_tok, spec_len, spec_seq, spec_seq, spec_seq, spec_seq, spec_vec, spec_mat, spec_vec, spec_mat, spec_vec, spec_head, spec_head, spec_head, spec_rows)
    return jax.shard_map(local_step, mesh=mesh, in_specs=in_specs, out_specs=(spec_tok, spec_seq, spec_seq), check_vma=False)
```

time: 440 us -> 295 us (0.67)
  matrix products: 195 us -> 0 us
  Pallas kernels: 0 us -> 194 us
  waiting for transfers between devices: 154 us -> 54 us
  other arithmetic: 33.4 us -> 8.08 us
  local copies, waits for them, and re-layouts: 42.2 us -> 23.7 us
  starting transfers between devices: 0.08 us -> 10.1 us
  between operations: 14.3 us -> 5 us
    pallas_call x0 -> x14, Pallas kernels: none -> 194 us  [the longest x8 76.3 us: out_proj(): pl.pallas_call(out_kernel, grid_spec=grid_spec, out_shape=[shape, shape],...]
    dot_general x7 -> x0, matrix products: 130 us -> none  [the longest x1 31.4 us: local_step(): jnp.einsum('bhts,bshv->bthv', attn_probs, values_all, preferred_element_t...]
    reduce_scatter x1 -> x0, waiting for transfers between devices: 103 us -> none  [local_step(): reduced = lax.psum_scatter(head_sum, 'tp', scatter_dimension=1, tiled=True)]
    sub x1 -> x0, matrix products: 64.6 us -> none  [local_step(): attn_probs = jax.nn.softmax(scores, axis=-1).astype(jnp.bfloat16)]
    ppermute x0 -> x15, waiting for transfers between devices: none -> 54 us  [local_step(): lax.ppermute(v, 'tp', [(i, i ^ bit) for i in range(4)])]
    all_gather x1 -> x0, waiting for transfers between devices: 50.6 us -> none  [local_step(): gathered = lax.all_gather(hidden, 'tp', axis=1, tiled=True)]
    dot_general x1 -> x0, local copies, waits for them, and re-layouts: 20.9 us -> none  [local_step(): jnp.einsum('bsc,chv->bshv', lat_all, w_uv, preferred_element_type=jnp.flo...]
    scatter x9 -> x0, other arithmetic: 20.7 us -> none
  transfers between devices with their start and end apart: 2 -> 15, of which waited for: 2 -> 3; matrix products, arithmetic and copies ran while one was open for 0% -> 5% of each run, Pallas kernels for 0% -> 42%
where the time goes in v1:
time: 295 us
  Pallas kernels  194 us (66%)
  waiting for transfers between devices  54 us (18%)
  local copies, waits for them, and re-layouts  23.7 us (8%)
  starting transfers between devices  10.1 us (3%)
  other arithmetic  8.08 us (3%)
  between operations  5 us (2%)
    pallas_call x8, Pallas kernels, out_proj(): pl.pallas_call(out_kernel, grid_spec=grid_spec, out_shape=[shape, shape],...  76.3 us
    pallas_call x2, Pallas kernels, attend(): pl.pallas_call(functools.partial(attn_kernel, seq), grid_spec=grid_spec,...  75.6 us
    ppermute x15, waiting for transfers between devices, local_step(): lax.ppermute(v, 'tp', [(i, i ^ bit) for i in range(4)])  54 us
    pallas_call x2, Pallas kernels, kv_up(): pl.pallas_call(functools.partial(kv_kernel, seq), grid_spec=grid_spec, ou...  27.4 us
    unnamed x70, local copies, waits for them, and re-layouts  13.7 us
    pallas_call x1, Pallas kernels, project(): pl.pallas_call(proj_kernel, grid=(dim // depth,), in_specs=[const((rows,...  13.4 us
    ppermute x15, starting transfers between devices, local_step(): lax.ppermute(v, 'tp', [(i, i ^ bit) for i in range(4)])  10.1 us
  transfers between devices with their start and end apart: 15, of which 3 were waited for; matrix products, arithmetic and copies ran while one was open for 5% of the time, Pallas kernels for 42%

profile of v1, /device:TPU:0, one launch (start us, length us, event | category | flops | bytes accessed | tf_op | source)
XLA Modules:
  0.0 295.0 jit_solution(13965348570509741195)
XLA Ops:
  0.7 5.0 %copy.26.c_ref = bf16[2,2304,512]{2,1,0:T(8,128)(2,1)} copy(bf16[2,2304,512]{2,1,0:T(8,128)(2,1)} %param.19) | data formatting | bytes 9437184
  5.7 0.8 copy.27
  6.8 3.3 %copy-done.12 = bf16[7168,576]{0,1:T(8,128)(2,1)S(1)} copy-done((bf16[7168,576]{0,1:T(8,128)(2,1)S(1)}, bf16[7168,576]{0,1:T(8,128)(2,1)}, u32[]{:S(2)}) %copy-start.12) | copy-done | bytes 8257560
  10.2 13.4 %project.1 = bf16[128,2176]{1,0:T(8,128)(2,1)S(1)} custom-call(bf16[128,7168]{1,0:T(8,128)(2,1)S(1)} %bitcast.30, f32[1,7168]{1,0:T(1,128)S(1)} %bitcast.38, bf16[7168,1536]{1,0:T(8,128)(2,1)} %wq_ref.1, bf16[576,7168]{1,0:T(8,128)(2,1)S(1)} %bitcast.33, f32[1,1536]{1,0:T(1,128)S(1)} %broadcast_in_dim.22.gq_ref, f32[1,512]{1,0:T(1,128)S(1)} %bitcast.39, ...), custom_call_target="tpu_custom_call" | custom-call | flops 11626610688 | bytes 30277632 | tf_op jit(solution)/shard_map/project/pallas_call | solution.py:70
  23.6 3.4 %collective-permute-start.1 = (bf16[2,64,2176]{2,1,0:T(8,128)(2,1)S(1)}, bf16[2,64,2176]{2,1,0:T(8,128)(2,1)S(1)}, u32[]{:S(2)}, u32[]{:S(2)}) collective-permute-start(bf16[2,64,2176]{2,1,0:T(8,128)(2,1)S(1)} %bitcast.34), channel_id=1, source_target_pairs={{0,2},{1,3},{2,0},{3,1},{4,6},{5,7},{6,4},{7,5}} | collective-permute-start | bytes 1671176 | tf_op jit(solution)/shard_map/ppermute | solution.py:275
  27.0 1.4 slice_bitcast_fusion.1
  28.3 1.4 prep.1
  29.8 13.9 %kv_up.2 = (bf16[2048,2048]{1,0:T(8,128)(2,1)}, bf16[2048,2048]{1,0:T(8,128)(2,1)}) custom-call(s32[2]{0:T(128)S(1)} %copy-done.11, bf16[2,2304,512]{2,1,0:T(8,128)(2,1)} %copy.26.c_ref, bf16[512,2048]{1,0:T(8,128)(2,1)S(1)} %get-tuple-element.31.wk_ref, bf16[2048,512]{1,0:T(8,128)(2,1)S(1)} %get-tuple-element.32.wvt_ref), custom_call_target="tpu_custom_call" | custom-call | flops 17179869184 | bytes 20971520 | tf_op jit(solution)/shard_map/kv_up/pallas_call | solution.py:142
  43.7 0.5 collective-permute-start.2
  44.2 13.5 %kv_up.3 = (bf16[2048,2048]{1,0:T(8,128)(2,1)}, bf16[2048,2048]{1,0:T(8,128)(2,1)}) custom-call(s32[2]{0:T(128)S(1)} %copy-done.11, bf16[2,2304,512]{2,1,0:T(8,128)(2,1)} %copy.26.c_ref, bf16[512,2048]{1,0:T(8,128)(2,1)S(1)} %get-tuple-element.31.wk_ref, bf16[2048,512]{1,0:T(8,128)(2,1)S(1)} %get-tuple-element.32.wvt_ref), custom_call_target="tpu_custom_call" | custom-call | flops 17179869184 | bytes 20971520 | tf_op jit(solution)/shard_map/kv_up/pallas_call | solution.py:142
  57.7 0.7 fusion
  62.5 0.4 copy-done.30
  62.9 0.4 copy-done.32
  63.3 0.2 copy-done.33
  63.6 37.7 %attend.2 = (bf16[256,2048]{1,0:T(8,128)(2,1)}, bf16[256,512]{1,0:T(8,128)(2,1)}, bf16[64,256]{1,0:T(8,128)(2,1)}) custom-call(s32[2]{0:T(128)} %len_ref.6, s32[4]{0:T(128)} %copy-done.30, bf16[2,64,2176]{2,1,0:T(8,128)(2,1)} %bitcast.36, bf16[2,64,2176]{2,1,0:T(8,128)(2,1)} %copy-done.32, bf16[2,64,2176]{2,1,0:T(8,128)(2,1)} %copy-done.31, ...), custom_call_target="tpu_custom_call" | custom-call | flops 19327352832 | bytes 33554432 | tf_op jit(solution)/shard_map/attend/pallas_call | solution.py:226
  101.3 1.2 copy-done.2
  102.5 9.8 %out_proj.11 = (f32[64,3584]{1,0:T(8,128)S(1)}, f32[64,3584]{1,0:T(8,128)}) custom-call(s32[2]{0:T(128)S(1)} %get-tuple-element.68.rows_ref, bf16[256,2048]{1,0:T(8,128)(2,1)S(1)} %copy-done.2, bf16[2048,7168]{1,0:T(8,128)(2,1)} %w_ref.15), custom_call_target="tpu_custom_call" | custom-call | flops 5637144576 | bytes 16777216 | tf_op jit(solution)/shard_map/out_proj/pallas_call | solution.py:262
  112.3 0.9 copy-done.7
  113.3 9.8 %out_proj.9 = (f32[64,3584]{1,0:T(8,128)S(1)}, f32[64,3584]{1,0:T(8,128)}) custom-call(s32[2]{0:T(128)S(1)} %get-tuple-element.68.rows_ref, bf16[256,2048]{1,0:T(8,128)(2,1)S(1)} %copy-done.2, bf16[2048,7168]{1,0:T(8,128)(2,1)} %w_ref.15), custom_call_target="tpu_custom_call" | custom-call | flops 5637144576 | bytes 16777216 | tf_op jit(solution)/shard_map/out_proj/pallas_call | solution.py:262
  123.1 0.5 collective-permute-start.4
  123.6 10.0 %out_proj.8 = (f32[64,3584]{1,0:T(8,128)S(1)}, f32[64,3584]{1,0:T(8,128)}) custom-call(s32[2]{0:T(128)S(1)} %get-tuple-element.67.rows_ref, bf16[256,2048]{1,0:T(8,128)(2,1)S(1)} %copy-done.2, bf16[2048,7168]{1,0:T(8,128)(2,1)} %w_ref.15), custom_call_target="tpu_custom_call" | custom-call | flops 5637144576 | bytes 16777216 | tf_op jit(solution)/shard_map/out_proj/pallas_call | solution.py:262
  133.6 1.9 dynamic_update_slice.12
  135.5 37.9 %attend.3 = (bf16[256,2048]{1,0:T(8,128)(2,1)}, bf16[256,512]{1,0:T(8,128)(2,1)}, bf16[64,256]{1,0:T(8,128)(2,1)}) custom-call(s32[2]{0:T(128)} %len_ref.6, s32[4]{0:T(128)} %copy-done.30, bf16[2,64,2176]{2,1,0:T(8,128)(2,1)} %bitcast.37, bf16[2,64,2176]{2,1,0:T(8,128)(2,1)} %copy-done.32, bf16[2,64,2176]{2,1,0:T(8,128)(2,1)} %copy-done.31, ...), custom_call_target="tpu_custom_call" | custom-call | flops 19327352832 | bytes 33554432 | tf_op jit(solution)/shard_map/attend/pallas_call | solution.py:226
  173.4 1.4 dynamic_update_slice.14
  174.8 1.2 copy-done
  176.0 9.8 %out_proj.15 = (f32[64,3584]{1,0:T(8,128)S(1)}, f32[64,3584]{1,0:T(8,128)}) custom-call(s32[2]{0:T(128)S(1)} %get-tuple-element.68.rows_ref, bf16[256,2048]{1,0:T(8,128)(2,1)S(1)} %copy-done, bf16[2048,7168]{1,0:T(8,128)(2,1)} %w_ref.15), custom_call_target="tpu_custom_call" | custom-call | flops 5637144576 | bytes 16777216 | tf_op jit(solution)/shard_map/out_proj/pallas_call | solution.py:262
  185.9 0.5 collective-permute-start.13
  186.4 9.8 %out_proj.10 = (f32[64,3584]{1,0:T(8,128)S(1)}, f32[64,3584]{1,0:T(8,128)}) custom-call(s32[2]{0:T(128)S(1)} %get-tuple-element.67.rows_ref, bf16[256,2048]{1,0:T(8,128)(2,1)S(1)} %copy-done.3, bf16[2048,7168]{1,0:T(8,128)(2,1)} %w_ref.15), custom_call_target="tpu_custom_call" | custom-call | flops 5637144576 | bytes 16777216 | tf_op jit(solution)/shard_map/out_proj/pallas_call | solution.py:262
  196.3 1.6 dynamic_update_slice.15
  198.0 2.8 dynamic_update_slice.13
  200.8 9.0 %out_proj.13 = (f32[64,3584]{1,0:T(8,128)S(1)}, f32[64,3584]{1,0:T(8,128)S(1)}) custom-call(s32[2]{0:T(128)S(1)} %get-tuple-element.68.rows_ref, bf16[256,2048]{1,0:T(8,128)(2,1)S(1)} %copy-done.1, bf16[2048,7168]{1,0:T(8,128)(2,1)} %w_ref.15), custom_call_target="tpu_custom_call" | custom-call | flops 5637144576 | bytes 16777216 | tf_op jit(solution)/shard_map/out_proj/pallas_call | solution.py:262
  209.8 0.4 collective-permute-start.10
  210.2 1.3 add.66
  211.5 0.8 collective-permute-start.8
  212.2 1.3 add.62
  213.5 1.3 collective-permute-start.5
  214.8 9.0 %out_proj.14 = (f32[64,3584]{1,0:T(8,128)S(1)}, f32[64,3584]{1,0:T(8,128)S(1)}) custom-call(s32[2]{0:T(128)S(1)} %get-tuple-element.67.rows_ref, bf16[256,2048]{1,0:T(8,128)(2,1)S(1)} %copy-done.1, bf16[2048,7168]{1,0:T(8,128)(2,1)} %w_ref.15), custom_call_target="tpu_custom_call" | custom-call | flops 5637144576 | bytes 16777216 | tf_op jit(solution)/shard_map/out_proj/pallas_call | solution.py:262
  223.9 9.0 %out_proj.12 = (f32[64,3584]{1,0:T(8,128)S(1)}, f32[64,3584]{1,0:T(8,128)S(1)}) custom-call(s32[2]{0:T(128)S(1)} %get-tuple-element.67.rows_ref, bf16[256,2048]{1,0:T(8,128)(2,1)S(1)} %copy-done.1, bf16[2048,7168]{1,0:T(8,128)(2,1)} %w_ref.15), custom_call_target="tpu_custom_call" | custom-call | flops 5637144576 | bytes 16777216 | tf_op jit(solution)/shard_map/out_proj/pallas_call | solution.py:262
  232.9 1.4 add.74
  234.4 0.5 collective-permute-start.9
  234.9 0.7 collective-permute-start.14
  235.7 1.3 collective-permute-start.11
  237.0 17.4 %collective-permute-done.5 = f32[64,3584]{1,0:T(8,128)S(1)} collective-permute-done((f32[64,3584]{1,0:T(8,128)S(1)}, f32[64,3584]{1,0:T(8,128)S(1)}, u32[]{:S(2)}, u32[]{:S(2)}) %collective-permute-start.5) | collective-permute-done | bytes 917536 | tf_op jit(solution)/shard_map/ppermute | solution.py:275
  254.4 1.9 add_convert_fusion.3
  256.4 17.6 %collective-permute-done.14 = f32[64,3584]{1,0:T(8,128)S(1)} collective-permute-done((f32[64,3584]{1,0:T(8,128)S(1)}, f32[64,3584]{1,0:T(8,128)S(1)}, u32[]{:S(2)}, u32[]{:S(2)}) %collective-permute-start.14) | collective-permute-done | bytes 917536 | tf_op jit(solution)/shard_map/ppermute | solution.py:275
  274.0 18.9 %collective-permute-done.11 = f32[64,3584]{1,0:T(8,128)S(1)} collective-permute-done((f32[64,3584]{1,0:T(8,128)S(1)}, f32[64,3584]{1,0:T(8,128)S(1)}, u32[]{:S(2)}, u32[]{:S(2)}) %collective-permute-start.11) | collective-permute-done | bytes 917536 | tf_op jit(solution)/shard_map/ppermute | solution.py:275
  293.0 0.6 add_convert_fusion.1
  293.6 1.4 pad_maximum_fusion
  (87 shorter events, 1.0 us)
Async XLA Ops:
  0.6 6.2 %copy-start.4 = (bf16[2,64,7168]{2,1,0:T(8,128)(2,1)S(1)}, bf16[2,64,7168]{2,1,0:T(8,128)(2,1)}, u32[]{:S(2)}) copy-start(bf16[2,64,7168]{2,1,0:T(8,128)(2,1)} %param.15) | copy-start | bytes 5505028
  0.6 5.9 %copy-start.28 = (f32[2,256,32]{1,2,0:T(8,128)S(1)}, f32[2,256,32]{1,2,0:T(8,128)}, u32[]{:S(2)}) copy-start(f32[2,256,32]{1,2,0:T(8,128)} %param.17) | copy-start | bytes 196612
  0.7 5.9 %copy-start.27 = (f32[2,256,32]{1,2,0:T(8,128)S(1)}, f32[2,256,32]{1,2,0:T(8,128)}, u32[]{:S(2)}) copy-start(f32[2,256,32]{1,2,0:T(8,128)} %param.18) | copy-start | bytes 196612
  0.7 5.0 %copy-start.22 = (bf16[2,2304,64]{1,2,0:T(8,128)(2,1)S(1)}, bf16[2,2304,64]{1,2,0:T(8,128)(2,1)}, u32[]{:S(2)}) copy-start(bf16[2,2304,64]{1,2,0:T(8,128)(2,1)} %param.20) | copy-start | bytes 1769476
  0.7 6.1 %copy-start.16 = (f32[7168]{0:T(1024)S(1)}, f32[7168]{0:T(1024)}, u32[]{:S(2)}) copy-start(f32[7168]{0:T(1024)} %param.21) | copy-start | bytes 86020
  0.7 6.1 %copy-start.29 = (f32[1536]{0:T(1024)S(1)}, f32[1536]{0:T(1024)}, u32[]{:S(2)}) copy-start(f32[1536]{0:T(1024)} %param.23) | copy-start | bytes 18436
  0.7 6.1 %copy-start.17 = (f32[512]{0:T(512)S(1)}, f32[512]{0:T(512)}, u32[]{:S(2)}) copy-start(f32[512]{0:T(512)} %param.25) | copy-start | bytes 6148
  6.8 3.3 %copy-start.12 = (bf16[7168,576]{0,1:T(8,128)(2,1)S(1)}, bf16[7168,576]{0,1:T(8,128)(2,1)}, u32[]{:S(2)}) copy-start(bf16[7168,576]{0,1:T(8,128)(2,1)} %param.24) | copy-start | bytes 24772612
  10.2 18.1 %copy-start.14 = (bf16[512,16,128]{2,1,0:T(8,128)(2,1)S(1)}, bf16[512,16,128]{2,1,0:T(8,128)(2,1)}, u32[]{:S(2)}) copy-start(bf16[512,16,128]{2,1,0:T(8,128)(2,1)} %wuv_ref.1) | copy-start | bytes 6291460
  23.6 6.2 %copy-start.15 = (bf16[128,2176]{1,0:T(8,128)(2,1)}, bf16[128,2176]{1,0:T(8,128)(2,1)S(1)}, u32[]{:S(2)}) copy-start(bf16[128,2176]{1,0:T(8,128)(2,1)S(1)} %project.1) | copy-start | bytes 1671172
  23.6 4.8 %copy-start.13 = (bf16[512,16,128]{2,1,0:T(8,128)(2,1)S(1)}, bf16[512,16,128]{2,1,0:T(8,128)(2,1)}, u32[]{:S(2)}) copy-start(bf16[512,16,128]{2,1,0:T(8,128)(2,1)} %wuk_ref.1) | copy-start | bytes 6291460
  23.6 20.1 %collective-permute-start.1 = (bf16[2,64,2176]{2,1,0:T(8,128)(2,1)S(1)}, bf16[2,64,2176]{2,1,0:T(8,128)(2,1)S(1)}, u32[]{:S(2)}, u32[]{:S(2)}) collective-permute-start(bf16[2,64,2176]{2,1,0:T(8,128)(2,1)S(1)} %bitcast.34), channel_id=1, source_target_pairs={{0,2},{1,3},{2,0},{3,1},{4,6},{5,7},{6,4},{7,5}} | collective-permute-start | bytes 1671176 | tf_op jit(solution)/shard_map/ppermute | solution.py:275
  26.9 35.6 %collective-permute-start = (bf16[2,64,2176]{2,1,0:T(8,128)(2,1)S(1)}, bf16[2,64,2176]{2,1,0:T(8,128)(2,1)S(1)}, u32[]{:S(2)}, u32[]{:S(2)}) collective-permute-start(bf16[2,64,2176]{2,1,0:T(8,128)(2,1)S(1)} %bitcast.35), channel_id=1, source_target_pairs={{0,1},{1,0},{2,3},{3,2},{4,5},{5,4},{6,7},{7,6}} | collective-permute-start | bytes 1671176 | tf_op jit(solution)/shard_map/ppermute | solution.py:275
  28.3 1.4 copy-start.11
  29.8 14.5 %copy-start.18 = (bf16[512,2048]{1,0:T(8,128)(2,1)}, bf16[512,2048]{1,0:T(8,128)(2,1)S(1)}, u32[]{:S(2)}) copy-start(bf16[512,2048]{1,0:T(8,128)(2,1)S(1)} %get-tuple-element.31.wk_ref) | copy-start | bytes 6291460
  29.8 14.5 %copy-start.19 = (bf16[2048,512]{1,0:T(8,128)(2,1)}, bf16[2048,512]{1,0:T(8,128)(2,1)S(1)}, u32[]{:S(2)}) copy-start(bf16[2048,512]{1,0:T(8,128)(2,1)S(1)} %get-tuple-element.32.wvt_ref) | copy-start | bytes 6291460
  43.7 14.1 %copy-start.31 = (bf16[2,64,2176]{2,1,0:T(8,128)(2,1)}, bf16[2,64,2176]{2,1,0:T(8,128)(2,1)S(1)}, u32[]{:S(2)}) copy-start(bf16[2,64,2176]{2,1,0:T(8,128)(2,1)S(1)} %collective-permute-done.1.b2) | copy-start | bytes 1671172
  43.7 18.8 %collective-permute-start.2 = (bf16[2,64,2176]{2,1,0:T(8,128)(2,1)S(1)}, bf16[2,64,2176]{2,1,0:T(8,128)(2,1)S(1)}, u32[]{:S(2)}, u32[]{:S(2)}) collective-permute-start(bf16[2,64,2176]{2,1,0:T(8,128)(2,1)S(1)} %collective-permute-done.1.b2), channel_id=1, source_target_pairs={{0,1},{1,0},{2,3},{3,2},{4,5},{5,4},{6,7},{7,6}} | collective-permute-start | bytes 1671176 | tf_op jit(solution)/shard_map/ppermute | solution.py:275
  62.5 0.8 copy-start.32
  62.5 1.0 copy-start.33
  101.3 1.2 copy-start.2
  112.3 0.9 copy-start.7
  123.1 10.5 %copy-start.5 = (f32[64,3584]{1,0:T(8,128)}, f32[64,3584]{1,0:T(8,128)S(1)}, u32[]{:S(2)}) copy-start(f32[64,3584]{1,0:T(8,128)S(1)} %get-tuple-element.38) | copy-start | bytes 2752516
  123.1 86.7 %collective-permute-start.7 = (f32[64,3584]{1,0:T(8,128)}, f32[64,3584]{1,0:T(8,128)}, u32[]{:S(2)}, u32[]{:S(2)}) collective-permute-start(f32[64,3584]{1,0:T(8,128)} %get-tuple-element.43), channel_id=1, source_target_pairs={{0,1},{1,0},{2,3},{3,2},{4,5},{5,4},{6,7},{7,6}} | collective-permute-start | bytes 2752520 | tf_op jit(solution)/shard_map/ppermute | solution.py:275
  123.1 88.4 %collective-permute-start.4 = (f32[64,3584]{1,0:T(8,128)}, f32[64,3584]{1,0:T(8,128)}, u32[]{:S(2)}, u32[]{:S(2)}) collective-permute-start(f32[64,3584]{1,0:T(8,128)} %get-tuple-element.39), channel_id=1, source_target_pairs={{0,1},{1,0},{2,3},{3,2},{4,5},{5,4},{6,7},{7,6}} | collective-permute-start | bytes 2752520 | tf_op jit(solution)/shard_map/ppermute | solution.py:275
  123.6 10.0 %copy-start.24 = (bf16[256,512]{1,0:T(8,128)(2,1)S(1)}, bf16[256,512]{1,0:T(8,128)(2,1)}, u32[]{:S(2)}) copy-start(bf16[256,512]{1,0:T(8,128)(2,1)} %get-tuple-element.55) | copy-start | bytes 786436
  133.6 100.8 %collective-permute-start.3 = (f32[64,3584]{1,0:T(8,128)}, f32[64,3584]{1,0:T(8,128)}, u32[]{:S(2)}, u32[]{:S(2)}) collective-permute-start(f32[64,3584]{1,0:T(8,128)} %get-tuple-element.37), channel_id=1, source_target_pairs={{0,1},{1,0},{2,3},{3,2},{4,5},{5,4},{6,7},{7,6}} | collective-permute-start | bytes 2752520 | tf_op jit(solution)/shard_map/ppermute | solution.py:275
  135.5 37.9 %copy-start.25 = (bf16[64,256]{1,0:T(8,128)(2,1)S(1)}, bf16[64,256]{1,0:T(8,128)(2,1)}, u32[]{:S(2)}) copy-start(bf16[64,256]{1,0:T(8,128)(2,1)} %get-tuple-element.57) | copy-start | bytes 98308
  174.8 1.2 copy-start
  176.0 10.4 %copy-start.3 = (bf16[256,2048]{1,0:T(8,128)(2,1)S(1)}, bf16[256,2048]{1,0:T(8,128)(2,1)}, u32[]{:S(2)}) copy-start(bf16[256,2048]{1,0:T(8,128)(2,1)} %get-tuple-element.35.o_ref) | copy-start | bytes 3145732
  185.8 10.3 %copy-start.9 = (f32[64,3584]{1,0:T(8,128)}, f32[64,3584]{1,0:T(8,128)S(1)}, u32[]{:S(2)}) copy-start(f32[64,3584]{1,0:T(8,128)S(1)} %get-tuple-element.53) | copy-start | bytes 2752516
  185.8 10.5 %copy-start.26 = (bf16[64,256]{1,0:T(8,128)(2,1)S(1)}, bf16[64,256]{1,0:T(8,128)(2,1)}, u32[]{:S(2)}) copy-start(bf16[64,256]{1,0:T(8,128)(2,1)} %get-tuple-element.58) | copy-start | bytes 98308
  185.8 12.1 %copy-start.23 = (bf16[256,512]{1,0:T(8,128)(2,1)S(1)}, bf16[256,512]{1,0:T(8,128)(2,1)}, u32[]{:S(2)}) copy-start(bf16[256,512]{1,0:T(8,128)(2,1)} %get-tuple-element.56) | copy-start | bytes 786436
  185.9 14.9 %copy-start.1 = (bf16[256,2048]{1,0:T(8,128)(2,1)S(1)}, bf16[256,2048]{1,0:T(8,128)(2,1)}, u32[]{:S(2)}) copy-start(bf16[256,2048]{1,0:T(8,128)(2,1)} %get-tuple-element.46.o_ref) | copy-start | bytes 3145732
  185.9 27.7 %collective-permute-start.13 = (f32[64,3584]{1,0:T(8,128)}, f32[64,3584]{1,0:T(8,128)}, u32[]{:S(2)}, u32[]{:S(2)}) collective-permute-start(f32[64,3584]{1,0:T(8,128)} %get-tuple-element.54), channel_id=1, source_target_pairs={{0,1},{1,0},{2,3},{3,2},{4,5},{5,4},{6,7},{7,6}} | collective-permute-start | bytes 2752520 | tf_op jit(solution)/shard_map/ppermute | solution.py:275
  196.2 38.7 %collective-permute-start.6 = (f32[64,3584]{1,0:T(8,128)}, f32[64,3584]{1,0:T(8,128)}, u32[]{:S(2)}, u32[]{:S(2)}) collective-permute-start(f32[64,3584]{1,0:T(8,128)} %get-tuple-element.41), channel_id=1, source_target_pairs={{0,1},{1,0},{2,3},{3,2},{4,5},{5,4},{6,7},{7,6}} | collective-permute-start | bytes 2752520 | tf_op jit(solution)/shard_map/ppermute | solution.py:275
  200.8 9.4 %copy-start.8 = (f32[64,3584]{1,0:T(8,128)S(1)}, f32[64,3584]{1,0:T(8,128)}, u32[]{:S(2)}) copy-start(f32[64,3584]{1,0:T(8,128)} %copy-done.7) | copy-start | bytes 2752516
  209.8 2.5 copy-start.6
  209.8 24.5 %collective-permute-start.10 = (f32[64,3584]{1,0:T(8,128)S(1)}, f32[64,3584]{1,0:T(8,128)S(1)}, u32[]{:S(2)}, u32[]{:S(2)}) collective-permute-start(f32[64,3584]{1,0:T(8,128)S(1)} %get-tuple-element.50), channel_id=1, source_target_pairs={{0,1},{1,0},{2,3},{3,2},{4,5},{5,4},{6,7},{7,6}} | collective-permute-start | bytes 2752520 | tf_op jit(solution)/shard_map/ppermute | solution.py:275
  211.5 24.2 %collective-permute-start.8 = (f32[64,3584]{1,0:T(8,128)S(1)}, f32[64,3584]{1,0:T(8,128)S(1)}, u32[]{:S(2)}, u32[]{:S(2)}) collective-permute-start(f32[64,3584]{1,0:T(8,128)S(1)} %add.66), channel_id=1, source_target_pairs={{0,2},{1,3},{2,0},{3,1},{4,6},{5,7},{6,4},{7,5}} | collective-permute-start | bytes 2752520 | tf_op jit(solution)/shard_map/ppermute | solution.py:275
  213.5 40.9 %collective-permute-start.5 = (f32[64,3584]{1,0:T(8,128)S(1)}, f32[64,3584]{1,0:T(8,128)S(1)}, u32[]{:S(2)}, u32[]{:S(2)}) collective-permute-start(f32[64,3584]{1,0:T(8,128)S(1)} %add.62), channel_id=1, source_target_pairs={{0,2},{1,3},{2,0},{3,1},{4,6},{5,7},{6,4},{7,5}} | collective-permute-start | bytes 2752520 | tf_op jit(solution)/shard_map/ppermute | solution.py:275
  223.9 9.0 %copy-start.10 = (f32[64,3584]{1,0:T(8,128)S(1)}, f32[64,3584]{1,0:T(8,128)}, u32[]{:S(2)}) copy-start(f32[64,3584]{1,0:T(8,128)} %copy-done.9) | copy-start | bytes 2752516
  232.9 21.5 %copy-start.21 = (bf16[64,7168]{1,0:T(8,128)(2,1)S(1)}, bf16[64,7168]{1,0:T(8,128)(2,1)}, u32[]{:S(2)}) copy-start(bf16[64,7168]{1,0:T(8,128)(2,1)} %get-tuple-element.59) | copy-start | bytes 2752516
  234.3 22.1 %collective-permute-start.12 = (f32[64,3584]{1,0:T(8,128)S(1)}, f32[64,3584]{1,0:T(8,128)S(1)}, u32[]{:S(2)}, u32[]{:S(2)}) collective-permute-start(f32[64,3584]{1,0:T(8,128)S(1)} %get-tuple-element.52), channel_id=1, source_target_pairs={{0,1},{1,0},{2,3},{3,2},{4,5},{5,4},{6,7},{7,6}} | collective-permute-start | bytes 2752520 | tf_op jit(solution)/shard_map/ppermute | solution.py:275
  234.4 22.0 %collective-permute-start.9 = (f32[64,3584]{1,0:T(8,128)S(1)}, f32[64,3584]{1,0:T(8,128)S(1)}, u32[]{:S(2)}, u32[]{:S(2)}) collective-permute-start(f32[64,3584]{1,0:T(8,128)S(1)} %get-tuple-element.48), channel_id=1, source_target_pairs={{0,1},{1,0},{2,3},{3,2},{4,5},{5,4},{6,7},{7,6}} | collective-permute-start | bytes 2752520 | tf_op jit(solution)/shard_map/ppermute | solution.py:275
  234.9 39.1 %collective-permute-start.14 = (f32[64,3584]{1,0:T(8,128)S(1)}, f32[64,3584]{1,0:T(8,128)S(1)}, u32[]{:S(2)}, u32[]{:S(2)}) collective-permute-start(f32[64,3584]{1,0:T(8,128)S(1)} %add.74), channel_id=1, source_target_pairs={{0,2},{1,3},{2,0},{3,1},{4,6},{5,7},{6,4},{7,5}} | collective-permute-start | bytes 2752520 | tf_op jit(solution)/shard_map/ppermute | solution.py:275
  235.7 57.3 %collective-permute-start.11 = (f32[64,3584]{1,0:T(8,128)S(1)}, f32[64,3584]{1,0:T(8,128)S(1)}, u32[]{:S(2)}, u32[]{:S(2)}) collective-permute-start(f32[64,3584]{1,0:T(8,128)S(1)} %add.70), channel_id=1, source_target_pairs={{0,2},{1,3},{2,0},{3,1},{4,6},{5,7},{6,4},{7,5}} | collective-permute-start | bytes 2752520 | tf_op jit(solution)/shard_map/ppermute | solution.py:275
  256.3 36.6 %copy-start.20 = (bf16[64,7168]{1,0:T(8,128)(2,1)S(1)}, bf16[64,7168]{1,0:T(8,128)(2,1)}, u32[]{:S(2)}) copy-start(bf16[64,7168]{1,0:T(8,128)(2,1)} %get-tuple-element.60) | copy-start | bytes 2752516
  (1 other events, 0.5 us)

commit v2 on v0

v2 whole, which is shorter than its diff:
```python
import functools

import jax
import jax.numpy as jnp
from jax import lax
from jax.experimental import pallas as pl
from jax.experimental.pallas import tpu as pltpu
from jax.sharding import PartitionSpec as P

F32 = jnp.float32
BF16 = jnp.bfloat16
EPS = 1e-6
MIB = 1 << 20
LAT_W = 2176
PREFIX = 2048
ROW_BLK = 512
CHUNK = 512
CHUNKS = 7168 // CHUNK
C2 = 192.0 ** -0.5 * 1.4426950408889634
NEG = -1e30
NT = (((1,), (1,)), ((), ()))


def dot(lhs, rhs):
    return jnp.dot(lhs, rhs, preferred_element_type=F32)


def dot_nt(lhs, rhs):
    return lax.dot_general(lhs, rhs, NT, preferred_element_type=F32)


def cost(flops, nbytes):
    return pl.CostEstimate(flops=int(flops), bytes_accessed=int(nbytes), transcendentals=0)


def proj_kernel(x_ref, g1_ref, wq_ref, wkvt_ref, gq_ref, gkv_ref, cos_ref, sin_ref, out_ref, a_s, q_acc, kv_acc):
    step = pl.program_id(0)
    depth = wq_ref.shape[0]

    @pl.when(step == 0)
    def _():
        xf = x_ref[...].astype(F32)
        inv = lax.rsqrt(jnp.mean(xf * xf, axis=-1, keepdims=True) + EPS)
        a_s[...] = (x_ref[...].astype(F32) * inv * g1_ref[...]).astype(BF16)
        q_acc[...] = jnp.zeros_like(q_acc)
        kv_acc[...] = jnp.zeros_like(kv_acc)

    a_blk = a_s[:, pl.ds(pl.multiple_of(step * depth, 128), depth)]
    q_acc[...] += dot(a_blk, wq_ref[...])
    kv_acc[...] += dot_nt(a_blk, wkvt_ref[...])

    @pl.when(step == pl.num_programs(0) - 1)
    def _():
        q = q_acc[...]
        inv = lax.rsqrt(jnp.mean(q * q, axis=-1, keepdims=True) + EPS)
        out_ref[:, :1536] = (q * inv * gq_ref[...]).astype(BF16)
        c = kv_acc[:, :512]
        inv = lax.rsqrt(jnp.mean(c * c, axis=-1, keepdims=True) + EPS)
        out_ref[:, 1536:2048] = (c * inv * gkv_ref[...]).astype(BF16)
        v1 = kv_acc[:, 512:544]
        v2 = kv_acc[:, 544:576]
        cos = cos_ref[...]
        sin = sin_ref[...]
        rot = jnp.concatenate([v1 * cos - v2 * sin, v2 * cos + v1 * sin, jnp.zeros((v1.shape[0], 64), F32)], axis=1)
        out_ref[:, 2048:] = rot.astype(BF16)


def project(x, g1, w_dq, w_dkvt, g_q, g_kv, cos, sin):
    rows, dim = x.shape
    depth = 1024
    const = lambda shape: pl.BlockSpec(shape, lambda k: (0,) * len(shape))
    return pl.pallas_call(
        proj_kernel,
        grid=(dim // depth,),
        in_specs=[
            const((rows, dim)),
            const((1, dim)),
            pl.BlockSpec((depth, 1536), lambda k: (k, 0)),
            pl.BlockSpec((576, depth), lambda k: (0, k)),
            const((1, 1536)),
            const((1, 512)),
            const((rows, 32)),
            const((rows, 32)),
        ],
        out_specs=const((rows, LAT_W)),
        out_shape=jax.ShapeDtypeStruct((rows, LAT_W), BF16),
        scratch_shapes=[pltpu.VMEM((rows, dim), BF16), pltpu.VMEM((rows, 1536), F32), pltpu.VMEM((rows, 576), F32)],
        compiler_params=pltpu.CompilerParams(vmem_limit_bytes=60 * MIB),
        cost_estimate=cost(2 * rows * dim * 2112 * 3, dim * 2112 * 2),
        name="project",
    )(x, g1, w_dq, w_dkvt, g_q, g_kv, cos, sin)


def prep_kernel(wuk_ref, wuv_ref, wk_ref, wvt_ref):
    wk_ref[...] = wuk_ref[...].reshape(wk_ref.shape)
    wvt_ref[...] = wuv_ref[...].reshape(wk_ref.shape).T


def prep_weights(w_uk, w_uv):
    rank, heads, dim = w_uk.shape
    blk = 256
    spec = pl.BlockSpec((blk, heads, dim), lambda i: (i, 0, 0))
    return pl.pallas_call(
        prep_kernel,
        grid=(rank // blk,),
        in_specs=[spec, spec],
        out_specs=[pl.BlockSpec((blk, heads * dim), lambda i: (i, 0)), pl.BlockSpec((heads * dim, blk), lambda i: (0, i))],
        out_shape=[jax.ShapeDtypeStruct((rank, heads * dim), BF16), jax.ShapeDtypeStruct((heads * dim, rank), BF16)],
        compiler_params=pltpu.CompilerParams(vmem_limit_bytes=40 * MIB),
        cost_estimate=cost(4e9, 8 * MIB),
        name="prep",
    )(w_uk, w_uv)


def cache_kernel(len_ref, c_ref, pe_ref, cn_ref, kn_ref, co_ref, po_ref):
    length = len_ref[pl.program_id(0)]
    base = pl.program_id(1) * 768
    row = lax.broadcasted_iota(jnp.int32, (768, 256), 0) + (base - length)
    hot = (row == lax.broadcasted_iota(jnp.int32, (768, 256), 1)).astype(F32).astype(BF16)
    row_c = lax.broadcasted_iota(jnp.int32, (768, 512), 0) + (base - length)
    new_c = dot(hot, cn_ref[...])
    co_ref[...] = jnp.where((row_c >= 0) & (row_c < 256), new_c, c_ref[...].astype(F32)).astype(BF16)
    col = lax.broadcasted_iota(jnp.int32, (64, 768), 1) + (base - length)
    new_p = dot_nt(kn_ref[...], hot)
    po_ref[...] = jnp.where((col >= 0) & (col < 256), new_p, pe_ref[...].astype(F32)).astype(BF16)


def update_caches(lengths, cache_lat, pe_t, c_new, k_newt):
    lat_spec = pl.BlockSpec((None, 768, 512), lambda b, r, n: (b, r, 0))
    pe_spec = pl.BlockSpec((None, 64, 768), lambda b, r, n: (b, 0, r))
    grid_spec = pltpu.PrefetchScalarGridSpec(
        num_scalar_prefetch=1,
        grid=(2, 3),
        in_specs=[
            lat_spec,
            pe_spec,
            pl.BlockSpec((None, 256, 512), lambda b, r, n: (b, 0, 0)),
            pl.BlockSpec((None, 64, 256), lambda b, r, n: (b, 0, 0)),
        ],
        out_specs=[lat_spec, pe_spec],
    )
    return pl.pallas_call(
        cache_kernel,
        grid_spec=grid_spec,
        out_shape=[jax.ShapeDtypeStruct(cache_lat.shape, BF16), jax.ShapeDtypeStruct(pe_t.shape, BF16)],
        compiler_params=pltpu.CompilerParams(vmem_limit_bytes=40 * MIB),
        cost_estimate=cost(4e9, 12 * MIB),
        name="caches",
    )(lengths, cache_lat, pe_t, c_new, k_newt)


def at(start, size, unit):
    return pl.ds(pl.multiple_of(start, unit), size)


def main_kernel(len_ref, lat, cos, sin, pet, c_hbm, wk_hbm, wvt_hbm, wq_hbm, wo_hbm, x_hbm,
                y_hbm, cnew_hbm, knewt_hbm,
                latb, cqa, cqt, cn, cnt, kn, knt, pe, mask, aug, cbuf, kb, vtb, wkb, wvtb, wqb, sb, mb, vb, ob, lhsb, wob,
                stage_d, xbuf, stage_x, rbuf, ownb, xres, ybuf,
                lat_send, lat_recv, c_sem, wk_sem, wvt_sem, wq_sem, wo_sem, x_sem, out_sem, y_sem,
                d_send, d_recv, i_send, i_recv, free_sem):
    me = lax.axis_index("tp")
    chip = me // 2
    core = me % 2
    sib = 2 * chip + (1 - core)
    far = 2 * (1 - chip) + core
    diag = 2 * (1 - chip) + (1 - core)

    def remote(src, dst, send, recv, peer):
        return pltpu.make_async_remote_copy(src_ref=src, dst_ref=dst, send_sem=send, recv_sem=recv, device_id={"tp": peer}, device_id_type=pl.DeviceIdType.MESH)

    def fetch_c(b):
        return pltpu.make_async_copy(c_hbm.at[b, pl.ds(0, PREFIX), :], cbuf, c_sem)

    def fetch_wq(h):
        return pltpu.make_async_copy(wq_hbm.at[h], wqb.at[h % 4], wq_sem.at[h % 4])

    def fetch_wo(g, n):
        return pltpu.make_async_copy(wo_hbm.at[:, at(n * CHUNK, CHUNK, CHUNK)], wob.at[g % 3], wo_sem.at[g % 3])

    copy_wk = pltpu.make_async_copy(wk_hbm, wkb, wk_sem)
    copy_wvt = pltpu.make_async_copy(wvt_hbm, wvtb, wvt_sem)
    copy_x = pltpu.make_async_copy(x_hbm, xres, x_sem)
    fetch_c(0).start()
    copy_wk.start()
    copy_wvt.start()

    barrier = pltpu.get_barrier_semaphore()
    for peer in (sib, far):
        pl.semaphore_signal(barrier, inc=1, device_id={"tp": peer}, device_id_type=pl.DeviceIdType.MESH)
    pl.semaphore_wait(barrier, 2)

    to_far = [remote(lat.at[b], latb.at[b, 1], lat_send.at[b, 1], lat_recv.at[b, 1], far) for b in range(2)]
    to_sib = [remote(lat.at[b], latb.at[b, 0], lat_send.at[b, 0], lat_recv.at[b, 0], sib) for b in range(2)]
    onward = [remote(latb.at[b, 1], latb.at[b, 2], lat_send.at[b, 2], lat_recv.at[b, 2], sib) for b in range(2)]
    to_far[0].start()
    to_sib[0].start()
    to_far[1].start()
    to_sib[1].start()
    for h in range(3):
        fetch_wq(h).start()
    for n in range(3):
        fetch_wo(n, n).start()
    copy_x.start()

    aug[...] = jnp.where(lax.broadcasted_iota(jnp.int32, (64, 256), 0) == 0, 1.0, 0.0).astype(BF16)
    causal = lax.broadcasted_iota(jnp.int32, (256, 256), 0) <= lax.broadcasted_iota(jnp.int32, (256, 256), 1)

    def keys_values(b, forward):
        length = len_ref[b]
        row = lax.broadcasted_iota(jnp.int32, (PREFIX, 128), 0)
        lane = lax.broadcasted_iota(jnp.int32, (PREFIX, 128), 1)
        old = row < length
        mask[...] = jnp.where(old, 1.0, 0.0).astype(BF16)
        rot = pet[b, :, :PREFIX].astype(F32).T
        rot = jnp.concatenate([rot, jnp.zeros_like(rot)], axis=1)
        pe[...] = jnp.where(old, rot, jnp.where(lane == 64, NEG, 0.0)).astype(BF16)
        fetch_c(b).wait()

        def block(r, carry):
            if forward is not None:
                @pl.when(r == 3)
                def _():
                    forward()
            rows = at(r * ROW_BLK, ROW_BLK, ROW_BLK)
            m = mask[rows, :]
            c = cbuf[rows, :] * jnp.concatenate([m, m, m, m], axis=1)
            kb[rows, :] = dot(c, wkb[...]).astype(BF16)
            vtb[:, rows] = dot_nt(wvtb[...], c).astype(BF16)
            return carry

        lax.fori_loop(0, PREFIX // ROW_BLK, block, 0)

    def assemble(b):
        for src, owner in ((lat.at[b], me), (latb.at[b, 0], sib), (latb.at[b, 1], far), (latb.at[b, 2], diag)):
            rows = at(owner * 64, 64, 64)
            cqa[rows, :] = src[:, :1536]
            cn[b, rows, :] = src[:, 1536:2048]
            kn[rows, :] = src[:, 2048:]
        cqt[...] = cqa[...].T
        cnt[...] = cn[b].T
        knt[b] = kn[...].T[:64]

    def attend(b):
        def head(h, carry):
            d = at(h * 128, 128, 128)
            fetch_wq(h).wait()
            cos_b = cos[b]
            sin_b = sin[b]
            q = dot(wqb[h % 4], cqt[...])
            v1 = q[128:160]
            v2 = q[160:192]
            qt = jnp.concatenate([q[:128].astype(BF16), (v1 * cos_b - v2 * sin_b).astype(BF16), (v2 * cos_b + v1 * sin_b).astype(BF16), aug[...]], axis=0)
            k_new = dot(cn[b], wkb[:, d]).astype(BF16)
            vb[...] = dot(wvtb[d, :], cnt[...]).astype(BF16)
            s = dot(jnp.concatenate([k_new, kn[...]], axis=1), qt)
            s = jnp.where(causal, s, NEG)
            sb[PREFIX:, :] = s
            m8 = jnp.max(s.reshape(32, 8, 256), axis=0)
            for c in range(PREFIX // 256):
                rows = slice(c * 256, c * 256 + 256)
                s = dot(jnp.concatenate([kb[rows, d], pe[rows, :]], axis=1), qt)
                sb[rows, :] = s
                m8 = jnp.maximum(m8, jnp.max(s.reshape(32, 8, 256), axis=0))
            mb[...] = m8

            @pl.when(h + 3 < 16)
            def _():
                fetch_wq(h + 3).start()

            m = jnp.max(mb[...], axis=0, keepdims=True) * C2
            l8 = jnp.zeros((8, 256), F32)
            for c in range(9):
                rows = slice(c * 256, c * 256 + 256)
                p = jnp.exp2(sb[rows, :] * C2 - m)
                sb[rows, :] = p
                l8 = l8 + jnp.sum(p.reshape(32, 8, 256), axis=0)
            inv = 1.0 / jnp.sum(l8, axis=0, keepdims=True)
            acc = None
            for c in range(9):
                rows = slice(c * 256, c * 256 + 256)
                p = (sb[rows, :] * inv).astype(BF16)
                t = dot(vtb[d, rows] if c < 8 else vb[...], p)
                acc = t if acc is None else acc + t
            ob[b, :, d] = acc.T.astype(BF16)
            return carry

        lax.fori_loop(0, 16, head, 0)

    def to_sibling(b, n):
        return remote(stage_d.at[n % 4], xbuf.at[b, n], d_send.at[n % 4], d_recv.at[b, n], sib)

    def over_link(b, n):
        return remote(stage_x.at[b, n], rbuf.at[b, n], i_send.at[b, n], i_recv.at[b, n], far)

    def put_y(b, n):
        return pltpu.make_async_copy(ybuf.at[b, n], y_hbm.at[b, :, at(n * CHUNK, CHUNK, CHUNK)], y_sem.at[b, n])

    def product(b, unit, first, second, n):
        g = unit * CHUNKS + n
        fetch_wo(g, n).wait()
        y = dot(lhsb[...], wob[g % 3])
        return y, g

    def next_wo(g):
        @pl.when(g + 3 < 4 * CHUNKS)
        def _():
            fetch_wo(g + 3, (g + 3) % CHUNKS).start()

    def load_lhs(b, first, second):
        lhsb[:64, :] = ob[b, at(first * 64, 64, 64), :]
        lhsb[64:, :] = ob[b, at(second * 64, 64, 64), :]

    def far_unit(b, unit):
        load_lhs(b, far, diag)

        def pass_on(n):
            to_sibling(b, n).wait_recv()
            stage_x[b, n] = stage_x[b, n] + xbuf[b, n]
            over_link(b, n).start()

        def chunk(n, carry):
            y, g = product(b, unit, far, diag, n)

            @pl.when(n >= 4)
            def _():
                to_sibling(b, n - 4).wait_send()

            stage_d[n % 4] = y[64:]
            stage_x[b, n] = y[:64]
            to_sibling(b, n).start()
            next_wo(g)

            @pl.when(n >= 1)
            def _():
                pass_on(n - 1)

            return carry

        lax.fori_loop(0, CHUNKS, chunk, 0)
        pass_on(CHUNKS - 1)
        for n in range(CHUNKS - 4, CHUNKS):
            to_sibling(b, n).wait_send()

    def own_unit(b, unit):
        load_lhs(b, me, sib)

        def finish(n):
            to_sibling(b, n).wait_recv()
            over_link(b, n).wait_recv()
            total = ownb[n % 2] + xbuf[b, n] + rbuf[b, n]
            ybuf[b, n] = (xres[b, :, at(n * CHUNK, CHUNK, CHUNK)].astype(F32) + total).astype(BF16)
            put_y(b, n).start()

        def chunk(n, carry):
            y, g = product(b, unit, me, sib, n)

            @pl.when(n >= 4)
            def _():
                to_sibling(b, n - 4).wait_send()

            stage_d[n % 4] = y[64:]
            ownb[n % 2] = y[:64]
            to_sibling(b, n).start()
            next_wo(g)

            @pl.when(n >= 1)
            def _():
                finish(n - 1)

            return carry

        lax.fori_loop(0, CHUNKS, chunk, 0)
        finish(CHUNKS - 1)
        for n in range(CHUNKS - 4, CHUNKS):
            to_sibling(b, n).wait_send()

    def forward_first():
        to_far[0].wait_recv()
        onward[0].start()

    copy_wk.wait()
    copy_wvt.wait()
    keys_values(0, forward_first)
    fetch_c(1).start()
    to_sib[0].wait_recv()
    onward[0].wait_recv()
    assemble(0)
    attend(0)
    for h in range(3):
        fetch_wq(h).start()
    to_far[1].wait_recv()
    onward[1].start()
    far_unit(0, 0)
    keys_values(1, None)
    to_sib[1].wait_recv()
    onward[1].wait_recv()
    assemble(1)
    put_c = pltpu.make_async_copy(cn, cnew_hbm, out_sem.at[0])
    put_k = pltpu.make_async_copy(knt, knewt_hbm, out_sem.at[1])
    put_c.start()
    put_k.start()
    attend(1)
    far_unit(1, 1)
    pl.semaphore_signal(free_sem, inc=1, device_id={"tp": sib}, device_id_type=pl.DeviceIdType.MESH)
    copy_x.wait()
    pl.semaphore_wait(free_sem, 1)
    own_unit(0, 2)
    own_unit(1, 3)
    for b in range(2):
        to_far[b].wait_send()
        to_sib[b].wait_send()
        onward[b].wait_send()

        def drain(n, carry):
            over_link(b, n).wait_send()
            put_y(b, n).wait()
            return carry

        lax.fori_loop(0, CHUNKS, drain, 0)
    put_c.wait()
    put_k.wait()


def main_call(lengths, lat, cos_t, sin_t, pe_t, cache_lat, wk, wvt, w_uqt, w_out, hidden):
    vmem = pl.BlockSpec(memory_space=pltpu.VMEM)
    hbm = pl.BlockSpec(memory_space=pl.ANY)
    dma = pltpu.SemaphoreType.DMA
    return pl.pallas_call(
        main_kernel,
        in_specs=[pl.BlockSpec(memory_space=pltpu.SMEM)] + [vmem] * 4 + [hbm] * 6,
        out_specs=[hbm] * 3,
        out_shape=[
            jax.ShapeDtypeStruct((2, 64, 7168), BF16),
            jax.ShapeDtypeStruct((2, 256, 512), BF16),
            jax.ShapeDtypeStruct((2, 64, 256), BF16),
        ],
        scratch_shapes=[
            pltpu.VMEM((2, 3, 64, LAT_W), BF16),
            pltpu.VMEM((256, 1536), BF16),
            pltpu.VMEM((1536, 256), BF16),
            pltpu.VMEM((2, 256, 512), BF16),
            pltpu.VMEM((512, 256), BF16),
            pltpu.VMEM((256, 128), BF16),
            pltpu.VMEM((2, 64, 256), BF16),
            pltpu.VMEM((PREFIX, 128), BF16),
            pltpu.VMEM((PREFIX, 128), BF16),
            pltpu.VMEM((64, 256), BF16),
            pltpu.VMEM((PREFIX, 512), BF16),
            pltpu.VMEM((PREFIX, 2048), BF16),
            pltpu.VMEM((2048, PREFIX), BF16),
            pltpu.VMEM((512, 2048), BF16),
            pltpu.VMEM((2048, 512), BF16),
            pltpu.VMEM((4, 192, 1536), BF16),
            pltpu.VMEM((PREFIX + 256, 256), F32),
            pltpu.VMEM((8, 256), F32),
            pltpu.VMEM((128, 256), BF16),
            pltpu.VMEM((2, 256, 2048), BF16),
            pltpu.VMEM((128, 2048), BF16),
            pltpu.VMEM((3, 2048, CHUNK), BF16),
            pltpu.VMEM((4, 64, CHUNK), F32),
            pltpu.VMEM((2, CHUNKS, 64, CHUNK), F32),
            pltpu.VMEM((2, CHUNKS, 64, CHUNK), F32),
            pltpu.VMEM((2, CHUNKS, 64, CHUNK), F32),
            pltpu.VMEM((2, 64, CHUNK), F32),
            pltpu.VMEM((2, 64, 7168), BF16),
            pltpu.VMEM((2, CHUNKS, 64, CHUNK), BF16),
            dma((2, 3)),
            dma((2, 3)),
            dma,
            dma,
            dma,
            dma((4,)),
            dma((3,)),
            dma,
            dma((2,)),
            dma((2, CHUNKS)),
            dma((4,)),
            dma((2, CHUNKS)),
            dma((2, CHUNKS)),
            dma((2, CHUNKS)),
            pltpu.SemaphoreType.REGULAR,
        ],
        compiler_params=pltpu.CompilerParams(vmem_limit_bytes=67043328, collective_id=0, has_side_effects=True),
        cost_estimate=cost(1e11, 200 * MIB),
        name="main",
    )(lengths, lat, cos_t, sin_t, pe_t, cache_lat, wk, wvt, w_uqt, w_out, hidden)


def solution(mesh):
    def local_step(hidden, lengths, rope_cos, rope_sin, cache_lat, cache_pe, norm_in, w_dq, norm_q, w_dkv, norm_kv, w_uq, w_uk, w_uv, w_out):
        me = lax.axis_index("tp")
        cos_t = jnp.swapaxes(rope_cos, 1, 2)
        sin_t = jnp.swapaxes(rope_sin, 1, 2)
        pe_t = jnp.swapaxes(cache_pe, 1, 2)
        w_uqt = jnp.transpose(w_uq, (1, 2, 0))
        own = lambda tab: lax.dynamic_slice_in_dim(tab, me * 64, 64, axis=1).reshape(128, 32)
        wk, wvt = prep_weights(w_uk, w_uv)
        lat = project(hidden.reshape(128, -1), norm_in[None], w_dq, w_dkv.T, norm_q[None], norm_kv[None], own(rope_cos), own(rope_sin))
        y, c_new, k_newt = main_call(lengths, lat.reshape(2, 64, LAT_W), cos_t, sin_t, pe_t, cache_lat, wk, wvt, w_uqt, w_out, hidden)
        lat_new, pe_new = update_caches(lengths, cache_lat, pe_t, c_new, k_newt)
        return y, lat_new, jnp.swapaxes(pe_new, 1, 2)

    spec_tok = P("dp", "tp", None)
    spec_len = P("dp")
    spec_seq = P("dp", None, None)
    spec_vec = P(None)
    spec_mat = P(None, None)
    spec_head = P(None, "tp", None)
    spec_rows = P("tp", None)
    in_specs = (spec_tok, spec_len, spec_seq, spec_seq, spec_seq, spec_seq, spec_vec, spec_mat, spec_vec, spec_mat, spec_vec, spec_head, spec_head, spec_head, spec_rows)
    return jax.shard_map(local_step, mesh=mesh, in_specs=in_specs, out_specs=(spec_tok, spec_seq, spec_seq), check_vma=False)
```

time: 440 us -> 182 us (0.41)
  matrix products: 195 us -> 0 us
  Pallas kernels: 0 us -> 166 us
  waiting for transfers between devices: 154 us -> 0 us
  other arithmetic: 33.4 us -> 0 us
  local copies, waits for them, and re-layouts: 42.2 us -> 15 us
  between operations: 14.3 us -> 0.68 us
    pallas_call x0 -> x4, Pallas kernels: none -> 166 us  [the longest x1 143 us: main_call(): pl.pallas_call(main_kernel, in_specs=[pl.BlockSpec(memory_space=pltpu.SME...]
    dot_general x7 -> x0, matrix products: 130 us -> none  [the longest x1 31.4 us: local_step(): jnp.einsum('bhts,bshv->bthv', attn_probs, values_all, preferred_element_t...]
    reduce_scatter x1 -> x0, waiting for transfers between devices: 103 us -> none  [local_step(): reduced = lax.psum_scatter(head_sum, 'tp', scatter_dimension=1, tiled=True)]
    sub x1 -> x0, matrix products: 64.6 us -> none  [local_step(): attn_probs = jax.nn.softmax(scores, axis=-1).astype(jnp.bfloat16)]
    all_gather x1 -> x0, waiting for transfers between devices: 50.6 us -> none  [local_step(): gathered = lax.all_gather(hidden, 'tp', axis=1, tiled=True)]
    dot_general x1 -> x0, local copies, waits for them, and re-layouts: 20.9 us -> none  [local_step(): jnp.einsum('bsc,chv->bshv', lat_all, w_uv, preferred_element_type=jnp.flo...]
    scatter x9 -> x0, other arithmetic: 20.7 us -> none
    scatter x16 -> x0, local copies, waits for them, and re-layouts: 13.8 us -> none
  transfers between devices with their start and end apart: 2 -> 0, of which waited for: 2 -> 0; matrix products, arithmetic and copies ran while one was open for 0% -> 0% of each run, Pallas kernels for 0% -> 0%
where the time goes in v2:
time: 182 us; the launch traced here: 181 us
  Pallas kernels  166 us (91%)
  local copies, waits for them, and re-layouts  15 us (8%)
    pallas_call x1, Pallas kernels, main_call(): pl.pallas_call(main_kernel, in_specs=[pl.BlockSpec(memory_space=pltpu.SME...  143 us
    pallas_call x1, Pallas kernels, project(): pl.pallas_call(proj_kernel, grid=(dim // depth,), in_specs=[const((rows,...  16.1 us
    unnamed x21, local copies, waits for them, and re-layouts  11.4 us
    pallas_call x1, Pallas kernels, update_caches(): pl.pallas_call(cache_kernel, grid_spec=grid_spec, out_shape=[jax.ShapeDty...  5.09 us

profile of v2, /device:TPU:0, one launch (start us, length us, event | category | flops | bytes accessed | tf_op | source)
XLA Modules:
  0.0 181.3 jit_solution(14615596502587588053)
XLA Ops:
  0.6 1.3 broadcast_in_dim.10.gq_ref
  1.9 0.8 constant_dynamic-slice_fusion
  2.8 0.7 copy.19
  3.5 0.7 copy.18
  4.2 0.0 copy-start.1
  4.2 16.1 %project.1 = bf16[128,2176]{1,0:T(8,128)(2,1)} custom-call(bf16[128,7168]{1,0:T(8,128)(2,1)} %bitcast.20, f32[1,7168]{1,0:T(1,128)} %bitcast.21, bf16[7168,1536]{1,0:T(8,128)(2,1)} %wq_ref.1, bf16[576,7168]{1,0:T(8,128)(2,1)} %bitcast.19, f32[1,1536]{1,0:T(1,128)} %broadcast_in_dim.10.gq_ref, f32[1,512]{1,0:T(1,128)} %bitcast.22, f32[128,32]{1,0:T(8,128)} %bitcast.15, ...), custom_call_target="tpu_custom_call" | custom-call | flops 11626610688 | bytes 30277632 | tf_op jit(solution)/shard_map/project/pallas_call | solution.py:72
  20.4 0.0 copy-done.1
  20.4 0.0 copy-start.2
  20.4 1.6 copy-done.2
  22.0 1.4 prep.1
  23.4 0.0 copy-start.5
  23.4 1.3 copy-done.5
  24.7 0.0 copy-start.6
  24.7 1.3 copy-done.6
  26.0 143.0 %main.1 = (bf16[2,64,7168]{2,1,0:T(8,128)(2,1)}, bf16[2,256,512]{2,1,0:T(8,128)(2,1)}, bf16[2,64,256]{2,1,0:T(8,128)(2,1)}) custom-call(s32[2]{0:T(128)} %len_ref.3, bf16[2,64,2176]{2,1,0:T(8,128)(2,1)} %bitcast.24, f32[2,32,256]{2,1,0:T(8,128)} %bitcast.17, f32[2,32,256]{2,1,0:T(8,128)} %bitcast.16, bf16[2,64,2304]{2,1,0:T(8,128)(2,1)} %bitcast.12, ...), custom_call_target="tpu_custom_call" | custom-call | flops 99999997952 | bytes 209715200 | tf_op jit(solution)/shard_map/main/pallas_call | solution.py:429
  169.1 0.0 copy-start
  169.1 2.3 %copy-done = bf16[2,2304,512]{2,1,0:T(8,128)(2,1)S(1)} copy-done((bf16[2,2304,512]{2,1,0:T(8,128)(2,1)S(1)}, bf16[2,2304,512]{2,1,0:T(8,128)(2,1)}, u32[]{:S(2)}) %copy-start) | copy-done | bytes 4718616
  171.4 0.0 copy-start.3
  171.4 1.1 copy-done.3
  172.5 0.0 copy-start.4
  172.5 0.7 copy-done.4
  173.1 0.0 copy-start.7
  173.1 1.0 copy-done.7
  174.2 0.0 copy-start.8
  174.2 0.8 copy-done.8
  175.0 0.0 copy-start.9
  175.0 5.1 %caches.1 = (bf16[2,2304,512]{2,1,0:T(8,128)(2,1)}, bf16[2,64,2304]{2,1,0:T(8,128)(2,1)}) custom-call(s32[2]{0:T(128)S(1)} %copy-done.4, bf16[2,2304,512]{2,1,0:T(8,128)(2,1)S(1)} %copy-done, bf16[2,64,2304]{2,1,0:T(8,128)(2,1)S(1)} %bitcast.13, bf16[2,256,512]{2,1,0:T(8,128)(2,1)S(1)} %copy-done.7, bf16[2,64,256]{2,1,0:T(8,128)(2,1)S(1)} %copy-done.8), custom_call_target="tpu_custom_call" | custom-call | flops 4000000000 | bytes 12582912 | tf_op jit(solution)/shard_map/caches/pallas_call | solution.py:142
  180.1 0.0 copy-done.9
  180.1 1.2 copy.21
Async XLA Ops:
  4.2 16.2 %copy-start.1 = (bf16[512,16,128]{2,1,0:T(8,128)(2,1)S(1)}, bf16[512,16,128]{2,1,0:T(8,128)(2,1)}, u32[]{:S(2)}) copy-start(bf16[512,16,128]{2,1,0:T(8,128)(2,1)} %wuk_ref.1) | copy-start | bytes 6291460
  20.4 1.6 copy-start.2
  23.4 1.3 copy-start.5
  24.7 1.3 copy-start.6
  169.1 2.3 %copy-start = (bf16[2,2304,512]{2,1,0:T(8,128)(2,1)S(1)}, bf16[2,2304,512]{2,1,0:T(8,128)(2,1)}, u32[]{:S(2)}) copy-start(bf16[2,2304,512]{2,1,0:T(8,128)(2,1)} %c_ref.1) | copy-start | bytes 14155780
  171.4 1.1 copy-start.3
  172.5 0.7 copy-start.4
  173.1 1.0 copy-start.7
  174.2 0.8 copy-start.8
  175.0 5.1 %copy-start.9 = (bf16[2,64,7168]{2,1,0:T(8,128)(2,1)S(1)}, bf16[2,64,7168]{2,1,0:T(8,128)(2,1)}, u32[]{:S(2)}) copy-start(bf16[2,64,7168]{2,1,0:T(8,128)(2,1)} %get-tuple-element.22) | copy-start | bytes 5505028
